TPU v7x, 8 devices: a whole 2x2x1 slice. The times are simulated.
8 devices in a mesh: dp: 1 (over z), yz: 2 (over y), x: 4 (over x, core).
Axes of the slice: x: 2, y: 2, z: 1, core: 2. Of those that a mesh axis runs over, the one named last changes fastest.
Arguments:
- h_in: bfloat16 [256, 1024], P('dp', ('x', 'yz'))
- seq_lens: int32 [256], P('dp')
- k_cache: bfloat16 [2, 256, 16, 512, 64], P(None, 'dp', ('yz', 'x'))
- v_cache: bfloat16 [2, 256, 16, 512, 64], P(None, 'dp', ('yz', 'x'))
- g_attn: bfloat16 [2, 1024], P(None, ('x', 'yz'))
- w_q: bfloat16 [2, 1024, 1024], P(None, 'x', 'yz')
- w_k: bfloat16 [2, 1024, 1024], P(None, 'x', 'yz')
- w_v: bfloat16 [2, 1024, 1024], P(None, 'x', 'yz')
- w_o: bfloat16 [2, 1024, 1024], P(None, 'yz', 'x')
- g_mlp: bfloat16 [2, 1024], P(None, ('x', 'yz'))
- w_in: bfloat16 [2, 1024, 2816], P(None, 'x', 'yz')
- w_out: bfloat16 [2, 2816, 1024], P(None, 'yz', 'x')
- g_final: bfloat16 [1024], P(('x', 'yz'))
- w_unemb: bfloat16 [1024, 32128], P('x', 'yz')
Outputs:
- output 1: bfloat16 [256, 1024], P('dp', ('x', 'yz'))
- output 2: float32 [256, 32128], P('dp', ('yz', 'x'))
- output 3: bfloat16 [2, 256, 16, 64], P(None, 'dp', ('yz', 'x'))
- output 4: bfloat16 [2, 256, 16, 64], P(None, 'dp', ('yz', 'x'))
All inputs are finite; a program needn't handle non-finite values.
Results may differ from a plain program's by a relative error of at most 0.0186626.
Values are sent between devices in bfloat16 or wider.
A program may use at most 1 GiB of HBM per device.

v0:
```python
import jax
import jax.numpy as jnp
from jax import lax
from jax.sharding import PartitionSpec as P

NORM_EPS = 1e-6


def attend(q_heads, k_new, v_new, k_cache, v_cache, seq_lens):
    inv_sqrt = q_heads.shape[-1] ** -0.5
    s_cache = jnp.einsum('bhd,bhsd->bhs', q_heads, k_cache, preferred_element_type=jnp.float32) * inv_sqrt
    s_new = jnp.einsum('bhd,bhd->bh', q_heads, k_new, preferred_element_type=jnp.float32) * inv_sqrt
    valid_pos = jnp.arange(k_cache.shape[2])[None, None, :] < seq_lens[:, None, None]
    s_cache = jnp.where(valid_pos, s_cache, -1e30)
    score_max = jnp.maximum(jnp.max(s_cache, axis=-1), s_new)
    p_cache = jnp.exp(s_cache - score_max[:, :, None])
    p_new = jnp.exp(s_new - score_max)
    prob_sum = jnp.sum(p_cache, axis=-1) + p_new
    p_cache = (p_cache / prob_sum[:, :, None]).astype(jnp.bfloat16)
    p_new = (p_new / prob_sum).astype(jnp.bfloat16)
    mixed_out = jnp.einsum('bhs,bhsd->bhd', p_cache, v_cache, preferred_element_type=jnp.float32)
    mixed_out = mixed_out + p_new.astype(jnp.float32)[:, :, None] * v_new.astype(jnp.float32)
    return mixed_out.astype(jnp.bfloat16)


def matmul_bf16(row_act, weight):
    return jnp.dot(row_act, weight, preferred_element_type=jnp.float32).astype(jnp.bfloat16)


def residual_add(h_act, delta_sum):
    return (h_act.astype(jnp.float32) + delta_sum.astype(jnp.float32)).astype(jnp.bfloat16)


def solution(mesh):
    x_size = mesh.shape['x']
    yz_size = mesh.shape['yz']
    group_axes = ('x', 'yz')

    def norm_shard(h_loc, gain_loc, model_dim):
        h_f32 = h_loc.astype(jnp.float32)
        sum_sq = lax.psum(jnp.sum(h_f32 * h_f32, axis=-1, keepdims=True), group_axes)
        inv_rms = lax.rsqrt(sum_sq / model_dim + NORM_EPS)
        return (h_f32 * inv_rms * gain_loc.astype(jnp.float32)).astype(jnp.bfloat16)

    def decode_step(h_loc, seq_lens, k_cache, v_cache, g_attn, w_q, w_k, w_v, w_o, g_mlp, w_in, w_out, g_final, w_unemb):
        batch_size = h_loc.shape[0]
        local_heads = k_cache.shape[2]
        head_dim = k_cache.shape[4]
        model_dim = h_loc.shape[1] * x_size * yz_size
        k_list = []
        v_list = []
        for layer_idx in range(w_q.shape[0]):
            normed = norm_shard(h_loc, g_attn[layer_idx], model_dim)
            row_block = lax.all_gather(normed, 'yz', axis=1, tiled=True)
            q_heads, k_new, v_new = [
                lax.psum_scatter(matmul_bf16(row_block, weight[layer_idx]), 'x', scatter_dimension=1, tiled=True).reshape(batch_size, local_heads, head_dim)
                for weight in (w_q, w_k, w_v)
            ]
            attn_heads = attend(q_heads, k_new, v_new, k_cache[layer_idx], v_cache[layer_idx], seq_lens)
            heads_row = lax.all_gather(attn_heads.reshape(batch_size, local_heads * head_dim), 'x', axis=1, tiled=True)
            attn_sum = lax.psum_scatter(matmul_bf16(heads_row, w_o[layer_idx]), 'yz', scatter_dimension=1, tiled=True)
            h_loc = residual_add(h_loc, attn_sum)
            normed = norm_shard(h_loc, g_mlp[layer_idx], model_dim)
            row_block = lax.all_gather(normed, 'yz', axis=1, tiled=True)
            up_sum = lax.psum_scatter(matmul_bf16(row_block, w_in[layer_idx]), 'x', scatter_dimension=1, tiled=True)
            hidden = jax.nn.gelu(up_sum.astype(jnp.float32)).astype(jnp.bfloat16)
            hidden_row = lax.all_gather(hidden, 'x', axis=1, tiled=True)
            down_sum = lax.psum_scatter(matmul_bf16(hidden_row, w_out[layer_idx]), 'yz', scatter_dimension=1, tiled=True)
            h_loc = residual_add(h_loc, down_sum)
            k_list.append(k_new)
            v_list.append(v_new)
        normed = norm_shard(h_loc, g_final, model_dim)
        row_block = lax.all_gather(normed, 'yz', axis=1, tiled=True)
        logits = lax.psum_scatter(matmul_bf16(row_block, w_unemb), 'x', scatter_dimension=1, tiled=True).astype(jnp.float32)
        return h_loc, logits, jnp.stack(k_list), jnp.stack(v_list)

    emb_spec = P('dp', ('x', 'yz'))
    gain_spec = P(None, ('x', 'yz'))
    cache_spec = P(None, 'dp', ('yz', 'x'), None, None)
    in_rows = P(None, 'x', 'yz')
    out_rows = P(None, 'yz', 'x')
    new_spec = P(None, 'dp', ('yz', 'x'), None)
    in_specs = (emb_spec, P('dp'), cache_spec, cache_spec, gain_spec, in_rows, in_rows, in_rows, out_rows, gain_spec, in_rows, out_rows, P(('x', 'yz')), P('x', 'yz'))
    out_specs = (emb_spec, P('dp', ('yz', 'x')), new_spec, new_spec)
    return jax.shard_map(decode_step, mesh=mesh, in_specs=in_specs, out_specs=out_specs, check_vma=False)
```

profile of v0, /device:TPU:0, one launch (start us, length us, event | category | flops | bytes accessed | tf_op | source)
XLA Modules:
  0.0 465.2 jit_solution(5607895097112807710)
XLA Ops:
  7.2 1.0 fusion.61
  8.2 25.1 %psum.35 = f32[256,1]{0,1:T(1,128)S(1)} all-reduce(f32[256,1]{0,1:T(1,128)S(1)} %bitcast.201), channel_id=1, replica_groups=mesh['dp'=1,'yz'=2,'x'=4] {'x','yz'}, use_global_device_ids=true, to_apply=%region_1.0 | all-reduce | flops 256 | bytes 2048 | tf_op jit(solution)/shard_map/psum | solution.py:41
  34.9 5.2 %all_gather.27 = bf16[256,256]{1,0:T(8,128)(2,1)S(1)} all-gather(bf16[256,128]{1,0:T(8,128)(2,1)S(1)} %fusion.63), channel_id=1, replica_groups=mesh['dp'=1,'yz'=2,'x'=4] {'yz'}, dimensions={1}, use_global_device_ids=true | all-gather | bytes 196608 | tf_op jit(solution)/shard_map/all_gather | solution.py:54
  40.2 1.2 convolution_convert_fusion.8
  42.3 1.2 convolution_convert_fusion.7
  44.4 1.2 convolution_convert_fusion.6
  47.3 10.2 %reduce-scatter.40.cloned.1.call-done = bf16[128,256]{1,0:T(8,128)(2,1)} async-done(((bf16[512,256]{1,0:T(8,128)(2,1)}), bf16[128,256]{1,0:T(8,128)(2,1)}) %reduce-scatter.40.cloned.1.call-update) | async-done | bytes 65552
  57.5 1.0 copy.60
  58.5 12.9 %fusion.6 = f32[256,2,1,512]{3,2,1,0:T(1,128)S(1)} fusion(bf16[256,2,64,1]{2,3,1,0:T(2,128)(2,1)S(1)} %copy.60, bf16[2,256,2,512,64]{3,4,2,1,0:T(8,128)(2,1)} %param.16), kind=kOutput, calls=%fused_computation.6 | convolution fusion | flops 33554432 | bytes 34668544 | tf_op jit(solution)/shard_map/bhd,bhsd->bhs/dot_general | solution.py:11
  71.7 2.6 reduce-scatter.42.cloned.1.call-done
  76.1 14.1 %fusion.4 = f32[256,2,1,64]{3,2,1,0:T(1,128)S(1)} fusion(bf16[2,256,2,512,64]{3,4,2,1,0:T(8,128)(2,1)} %param.17, bf16[256,2,512,1]{2,0,1,3:T(8,128)(2,1)S(1)} %fusion.28), kind=kOutput, calls=%fused_computation.4 | convolution fusion | flops 33554432 | bytes 34209792 | tf_op jit(solution)/shard_map/bhs,bhsd->bhd/dot_general | solution.py:21
  90.4 1.5 reduce-scatter.44.cloned.1.call-done
  92.7 7.7 %all_gather.28 = bf16[256,512]{0,1:T(8,128)(2,1)S(1)} all-gather(bf16[256,128]{0,1:T(8,128)(2,1)S(1)} %bitcast.182), channel_id=1, replica_groups=mesh['dp'=1,'yz'=2,'x'=4] {'x'}, dimensions={1}, use_global_device_ids=true | all-gather | bytes 327680 | tf_op jit(solution)/shard_map/all_gather | solution.py:60
  100.5 1.2 convolution_convert_fusion.10
  102.5 8.8 %reduce-scatter.46.cloned.1.call-done = bf16[128,256]{1,0:T(8,128)(2,1)} async-done(((bf16[256,256]{1,0:T(8,128)(2,1)}), bf16[128,256]{1,0:T(8,128)(2,1)}) %reduce-scatter.46.cloned.1.call-update) | async-done | bytes 65552
  111.3 0.9 copy.83
  112.4 22.3 %psum.36 = f32[256,1]{0,1:T(1,128)S(1)} all-reduce(f32[256,1]{0,1:T(1,128)S(1)} %bitcast.202), channel_id=1, replica_groups=mesh['dp'=1,'yz'=2,'x'=4] {'x','yz'}, use_global_device_ids=true, to_apply=%region_9.10 | all-reduce | flops 256 | bytes 2048 | tf_op jit(solution)/shard_map/psum | solution.py:41
  134.8 5.2 %all_gather.29 = bf16[256,256]{1,0:T(8,128)(2,1)S(1)} all-gather(bf16[256,128]{1,0:T(8,128)(2,1)S(1)} %fusion.67), channel_id=1, replica_groups=mesh['dp'=1,'yz'=2,'x'=4] {'yz'}, dimensions={1}, use_global_device_ids=true | all-gather | bytes 196608 | tf_op jit(solution)/shard_map/all_gather | solution.py:64
  140.0 1.3 convolution_convert_fusion.2
  141.4 18.8 %reduce-scatter.34.cloned.1.call-done = bf16[256,352]{0,1:T(8,128)(2,1)} async-done(((bf16[256,1408]{0,1:T(8,128)(2,1)}), bf16[256,352]{0,1:T(8,128)(2,1)}) %reduce-scatter.34.cloned.1.call-update) | async-done | bytes 180240 | tf_op jit(solution)/shard_map/reduce_scatter | solution.py:65
  160.1 1.0 fusion.35
  161.2 10.9 %all_gather.30 = bf16[256,1408]{0,1:T(8,128)(2,1)S(1)} all-gather(bf16[256,352]{0,1:T(8,128)(2,1)S(1)} %fusion.35), channel_id=1, replica_groups=mesh['dp'=1,'yz'=2,'x'=4] {'x'}, dimensions={1}, use_global_device_ids=true | all-gather | bytes 901120 | tf_op jit(solution)/shard_map/all_gather | solution.py:67
  172.1 1.5 convolution_convert_fusion.12
  174.5 7.5 %reduce-scatter.48.cloned.1.call-done = bf16[128,256]{1,0:T(8,128)(2,1)} async-done(((bf16[256,256]{1,0:T(8,128)(2,1)}), bf16[128,256]{1,0:T(8,128)(2,1)}) %reduce-scatter.48.cloned.1.call-update) | async-done | bytes 65552
  183.1 22.3 %psum.37 = f32[256,1]{0,1:T(1,128)S(1)} all-reduce(f32[256,1]{0,1:T(1,128)S(1)} %bitcast.196), channel_id=1, replica_groups=mesh['dp'=1,'yz'=2,'x'=4] {'x','yz'}, use_global_device_ids=true, to_apply=%region_13.14 | all-reduce | flops 256 | bytes 2048 | tf_op jit(solution)/shard_map/psum | solution.py:41
  205.5 5.2 %all_gather.31 = bf16[256,256]{1,0:T(8,128)(2,1)S(1)} all-gather(bf16[256,128]{1,0:T(8,128)(2,1)S(1)} %fusion.71), channel_id=1, replica_groups=mesh['dp'=1,'yz'=2,'x'=4] {'yz'}, dimensions={1}, use_global_device_ids=true | all-gather | bytes 196608 | tf_op jit(solution)/shard_map/all_gather | solution.py:54
  213.0 1.2 convolution_convert_fusion.3
  215.2 12.6 %reduce-scatter.50.cloned.1.call-done = bf16[128,256]{1,0:T(8,128)(2,1)} async-done(((bf16[512,256]{1,0:T(8,128)(2,1)}), bf16[128,256]{1,0:T(8,128)(2,1)}) %reduce-scatter.50.cloned.1.call-update) | async-done | bytes 65552
  227.9 1.0 copy.67
  228.9 12.9 %fusion.2 = f32[256,2,1,512]{3,2,1,0:T(1,128)S(1)} fusion(bf16[256,2,64,1]{2,3,1,0:T(2,128)(2,1)S(1)} %copy.67, bf16[2,256,2,512,64]{3,4,2,1,0:T(8,128)(2,1)} %param.16), kind=kOutput, calls=%fused_computation.2 | convolution fusion | flops 33554432 | bytes 34668544 | tf_op jit(solution)/shard_map/bhd,bhsd->bhs/dot_general | solution.py:11
  242.1 2.6 reduce-scatter.52.cloned.1.call-done
  246.5 14.1 %fusion = f32[256,2,1,64]{3,2,1,0:T(1,128)S(1)} fusion(bf16[2,256,2,512,64]{3,4,2,1,0:T(8,128)(2,1)} %param.17, bf16[256,2,512,1]{2,0,1,3:T(8,128)(2,1)S(1)} %fusion.29), kind=kOutput, calls=%fused_computation | convolution fusion | flops 33554432 | bytes 34209792 | tf_op jit(solution)/shard_map/bhs,bhsd->bhd/dot_general | solution.py:21
  260.7 1.5 reduce-scatter.54.cloned.1.call-done
  263.1 7.8 %all_gather.32 = bf16[256,512]{0,1:T(8,128)(2,1)S(1)} all-gather(bf16[256,128]{0,1:T(8,128)(2,1)S(1)} %bitcast.183), channel_id=1, replica_groups=mesh['dp'=1,'yz'=2,'x'=4] {'x'}, dimensions={1}, use_global_device_ids=true | all-gather | bytes 327680 | tf_op jit(solution)/shard_map/all_gather | solution.py:60
  272.0 8.8 %reduce-scatter.56.cloned.1.call-done = bf16[128,256]{1,0:T(8,128)(2,1)} async-done(((bf16[256,256]{1,0:T(8,128)(2,1)}), bf16[128,256]{1,0:T(8,128)(2,1)}) %reduce-scatter.56.cloned.1.call-update) | async-done | bytes 65552
  281.9 22.3 %psum.38 = f32[256,1]{0,1:T(1,128)S(1)} all-reduce(f32[256,1]{0,1:T(1,128)S(1)} %bitcast.203), channel_id=1, replica_groups=mesh['dp'=1,'yz'=2,'x'=4] {'x','yz'}, use_global_device_ids=true, to_apply=%region_21.22 | all-reduce | flops 256 | bytes 2048 | tf_op jit(solution)/shard_map/psum | solution.py:41
  304.3 5.2 %all_gather.33 = bf16[256,256]{1,0:T(8,128)(2,1)S(1)} all-gather(bf16[256,128]{1,0:T(8,128)(2,1)S(1)} %fusion.75), channel_id=1, replica_groups=mesh['dp'=1,'yz'=2,'x'=4] {'yz'}, dimensions={1}, use_global_device_ids=true | all-gather | bytes 196608 | tf_op jit(solution)/shard_map/all_gather | solution.py:64
  309.5 1.3 convolution_convert_fusion.1
  310.9 18.7 %reduce-scatter.36.cloned.1.call-done = bf16[256,352]{0,1:T(8,128)(2,1)} async-done(((bf16[256,1408]{0,1:T(8,128)(2,1)}), bf16[256,352]{0,1:T(8,128)(2,1)}) %reduce-scatter.36.cloned.1.call-update) | async-done | bytes 180240 | tf_op jit(solution)/shard_map/reduce_scatter | solution.py:65
  329.6 1.0 fusion.41
  330.6 10.9 %all_gather.34 = bf16[256,1408]{0,1:T(8,128)(2,1)S(1)} all-gather(bf16[256,352]{0,1:T(8,128)(2,1)S(1)} %fusion.41), channel_id=1, replica_groups=mesh['dp'=1,'yz'=2,'x'=4] {'x'}, dimensions={1}, use_global_device_ids=true | all-gather | bytes 901120 | tf_op jit(solution)/shard_map/all_gather | solution.py:67
  341.5 1.5 convolution_convert_fusion.11
  343.9 7.5 %reduce-scatter.58.cloned.1.call-done = bf16[128,256]{1,0:T(8,128)(2,1)} async-done(((bf16[256,256]{1,0:T(8,128)(2,1)}), bf16[128,256]{1,0:T(8,128)(2,1)}) %reduce-scatter.58.cloned.1.call-update) | async-done | bytes 65552
  352.5 22.3 %psum.39 = f32[256,1]{0,1:T(1,128)S(1)} all-reduce(f32[256,1]{0,1:T(1,128)S(1)} %bitcast.194), channel_id=1, replica_groups=mesh['dp'=1,'yz'=2,'x'=4] {'x','yz'}, use_global_device_ids=true, to_apply=%region_25.26 | all-reduce | flops 256 | bytes 2048 | tf_op jit(solution)/shard_map/psum | solution.py:41
  374.9 5.2 %all_gather.35 = bf16[256,256]{1,0:T(8,128)(2,1)S(1)} all-gather(bf16[256,128]{1,0:T(8,128)(2,1)S(1)} %fusion.60), channel_id=1, replica_groups=mesh['dp'=1,'yz'=2,'x'=4] {'yz'}, dimensions={1}, use_global_device_ids=true | all-gather | bytes 196608 | tf_op jit(solution)/shard_map/all_gather | solution.py:73
  380.1 8.9 %convolution_convert_fusion = bf16[256,16064]{0,1:T(8,128)(2,1)} fusion(bf16[256,256]{1,0:T(8,128)(2,1)S(1)} %all_gather.35, bf16[256,16064]{0,1:T(8,128)(2,1)} %param.27), kind=kOutput, calls=%fused_computation.12 | convolution fusion | flops 2109652992 | bytes 16580608 | tf_op jit(solution)/shard_map/dot_general | solution.py:27
  391.2 63.6 %reduce-scatter.38.cloned.1.call-done = bf16[256,4016]{0,1:T(8,128)(2,1)} async-done(((bf16[256,16064]{0,1:T(8,128)(2,1)}), bf16[256,4016]{0,1:T(8,128)(2,1)}) %reduce-scatter.38.cloned.1.call-update) | async-done | bytes 2056208 | tf_op jit(solution)/shard_map/reduce_scatter | solution.py:74
  454.8 3.9 convert_element_type.207
  (106 shorter events, 24.4 us)
Async XLA Ops:
  7.2 50.3 %reduce-scatter.40.cloned.1.call-start = ((), (), s32[]{:S(2)}) async-start(), calls=%async_computation.16 | async-start | bytes 327680
  42.2 32.1 %reduce-scatter.42.cloned.1.call-start = ((), (), s32[]{:S(2)}) async-start(), calls=%async_computation.17 | async-start | bytes 327680
  44.3 47.5 %reduce-scatter.44.cloned.1.call-start = ((), (), s32[]{:S(2)}) async-start(), calls=%async_computation.18 | async-start | bytes 327680
  46.4 64.9 %reduce-scatter.46.cloned.1.call-start = ((), (), s32[]{:S(2)}) async-start(), calls=%async_computation.19 | async-start | bytes 196608
  58.5 15.9 %copy-start.4 = (bf16[128,256]{1,0:T(8,128)(2,1)S(1)}, bf16[128,256]{1,0:T(8,128)(2,1)}, u32[]{:S(2)}) copy-start(bf16[128,256]{1,0:T(8,128)(2,1)} %reduce-scatter.40.cloned.1.call-done) | copy-start | bytes 196612
  76.1 26.4 %copy-start.11 = (bf16[2,128]{1,0:T(2,128)(2,1)S(1)}, bf16[2,128]{1,0:T(2,128)(2,1)}, u32[]{:S(2)}) copy-start(bf16[2,128]{1,0:T(2,128)(2,1)} %param.23) | copy-start | bytes 1540
  76.1 36.2 %copy-start = (bf16[256,128]{1,0:T(8,128)(2,1)S(1)}, bf16[256,128]{1,0:T(8,128)(2,1)}, u32[]{:S(2)}) copy-start(bf16[256,128]{1,0:T(8,128)(2,1)} %param.14) | copy-start | bytes 196612
  76.1 63.9 %copy-start.1 = (bf16[2,256,1408]{2,1,0:T(8,128)(2,1)S(1)}, bf16[2,256,1408]{2,1,0:T(8,128)(2,1)}, u32[]{:S(2)}) copy-start(bf16[2,256,1408]{2,1,0:T(8,128)(2,1)} %param.24) | copy-start | bytes 4325380
  90.2 120.4 %copy-start.2 = (bf16[2,256,512]{2,1,0:T(8,128)(2,1)S(1)}, bf16[2,256,512]{2,1,0:T(8,128)(2,1)}, u32[]{:S(2)}) copy-start(bf16[2,256,512]{2,1,0:T(8,128)(2,1)} %param.19) | copy-start | bytes 1572868
  90.3 121.6 %copy-start.3 = (bf16[2,256,512]{2,1,0:T(8,128)(2,1)S(1)}, bf16[2,256,512]{2,1,0:T(8,128)(2,1)}, u32[]{:S(2)}) copy-start(bf16[2,256,512]{2,1,0:T(8,128)(2,1)} %param.20) | copy-start | bytes 1572868
  102.5 57.7 %reduce-scatter.34.cloned.1.call-start = ((), (), s32[]{:S(2)}) async-start(), calls=%async_computation.13 | async-start | bytes 901120 | tf_op jit(solution)/shard_map/reduce_scatter | solution.py:65
  141.3 40.7 %reduce-scatter.48.cloned.1.call-start = ((), (), s32[]{:S(2)}) async-start(), calls=%async_computation.20 | async-start | bytes 196608
  174.4 53.5 %reduce-scatter.50.cloned.1.call-start = ((), (), s32[]{:S(2)}) async-start(), calls=%async_computation.21 | async-start | bytes 327680
  211.8 33.0 %reduce-scatter.52.cloned.1.call-start = ((), (), s32[]{:S(2)}) async-start(), calls=%async_computation.22 | async-start | bytes 327680
  212.9 49.4 %reduce-scatter.54.cloned.1.call-start = ((), (), s32[]{:S(2)}) async-start(), calls=%async_computation.23 | async-start | bytes 327680
  215.0 65.8 %reduce-scatter.56.cloned.1.call-start = ((), (), s32[]{:S(2)}) async-start(), calls=%async_computation.24 | async-start | bytes 196608
  228.9 15.9 %copy-start.5 = (bf16[128,256]{1,0:T(8,128)(2,1)S(1)}, bf16[128,256]{1,0:T(8,128)(2,1)}, u32[]{:S(2)}) copy-start(bf16[128,256]{1,0:T(8,128)(2,1)} %reduce-scatter.50.cloned.1.call-done) | copy-start | bytes 196612
  246.5 24.4 %copy-start.12 = (bf16[2,512,256]{2,1,0:T(8,128)(2,1)S(1)}, bf16[2,512,256]{2,1,0:T(8,128)(2,1)}, u32[]{:S(2)}) copy-start(bf16[2,512,256]{2,1,0:T(8,128)(2,1)} %param.22) | copy-start | bytes 1572868
  260.6 83.3 %copy-start.13 = (bf16[128]{0:T(256)(128)(2,1)S(1)}, bf16[128]{0:T(256)(128)(2,1)}, u32[]{:S(2)}) copy-start(bf16[128]{0:T(256)(128)(2,1)} %param.26) | copy-start | bytes 772
  272.0 57.6 %reduce-scatter.36.cloned.1.call-start = ((), (), s32[]{:S(2)}) async-start(), calls=%async_computation.14 | async-start | bytes 901120 | tf_op jit(solution)/shard_map/reduce_scatter | solution.py:65
  310.8 40.6 %reduce-scatter.58.cloned.1.call-start = ((), (), s32[]{:S(2)}) async-start(), calls=%async_computation.25 | async-start | bytes 196608
  343.9 111.0 %reduce-scatter.38.cloned.1.call-start = ((), (), s32[]{:S(2)}) async-start(), calls=%async_computation.15 | async-start | bytes 10280960 | tf_op jit(solution)/shard_map/reduce_scatter | solution.py:74
  352.5 36.5 %copy-start.8 = (bf16[256,128]{1,0:T(8,128)(2,1)}, bf16[256,128]{1,0:T(8,128)(2,1)S(1)}, u32[]{:S(2)}) copy-start(bf16[256,128]{1,0:T(8,128)(2,1)S(1)} %get-tuple-element.5) | copy-start | bytes 196612
  389.0 0.8 copy-start.9
  389.0 0.9 copy-start.10
  389.0 1.5 copy-start.6
  389.0 1.5 copy-start.7
Sparse Core Ops, SparseCore 0:
  42.3 15.0 reduce-scatter.39
  59.9 14.4 reduce-scatter.41
  77.4 14.4 reduce-scatter.43
  102.6 8.6 reduce-scatter.45
  141.5 18.6 reduce-scatter.33
  174.5 7.4 reduce-scatter.47
  211.9 15.9 reduce-scatter.49
  230.3 14.4 reduce-scatter.51
  247.8 14.4 reduce-scatter.53
  272.1 8.6 reduce-scatter.55
  310.9 18.6 reduce-scatter.35
  344.0 7.4 reduce-scatter.57
  389.2 65.6 reduce-scatter.37
where the time goes:
time: 467 us; the launch traced here: 465 us
  blocking collectives  178 us (38%)
  waiting for transfers between devices  165 us (35%)
  matrix products  75 us (16%)
  other arithmetic  17.6 us (4%)
  local copies, waits for them, and re-layouts  15 us (3%)
  between operations  14.3 us (3%)
    psum x5, blocking collectives, norm_shard(): lax.psum(jnp.sum(h_f32 * h_f32, axis=-1, keepdims=True), group_axes)  114 us
    unnamed x23, waiting for transfers between devices  63.9 us
    reduce_scatter x1, waiting for transfers between devices, decode_step(): lax.psum_scatter(matmul_bf16(row_block, w_unemb), 'x', scatter_dimension=...  63.6 us
    reduce_scatter x2, waiting for transfers between devices, decode_step(): lax.psum_scatter(matmul_bf16(row_block, w_in[layer_idx]), 'x', scatter_di...  37.5 us
    dot_general x2, matrix products, attend(): jnp.einsum('bhs,bhsd->bhd', p_cache, v_cache, preferred_element_type=jnp....  28.2 us
    all_gather x5, blocking collectives, decode_step(): row_block = lax.all_gather(normed, 'yz', axis=1, tiled=True)  26.2 us
    dot_general x2, matrix products, attend(): jnp.einsum('bhd,bhsd->bhs', q_heads, k_cache, preferred_element_type=jnp....  25.7 us
    all_gather x2, blocking collectives, decode_step(): hidden_row = lax.all_gather(hidden, 'x', axis=1, tiled=True)  21.8 us
  transfers between devices with their start and end apart: 13, of which 13 were waited for; matrix products, arithmetic and copies ran while one was open for 15% of the time, Pallas kernels for 0%

commit v1 on v0

v1 whole, which is shorter than its diff:
```python
import functools

import jax
import jax.numpy as jnp
from jax import lax
from jax.experimental import pallas as pl
from jax.experimental.pallas import tpu as pltpu
from jax.sharding import PartitionSpec as P

NORM_EPS = 1e-6
MESH = pl.DeviceIdType.MESH
BF = jnp.bfloat16
F32 = jnp.float32
ANY = pl.BlockSpec(memory_space=pl.ANY)
VM = pl.BlockSpec(memory_space=pltpu.VMEM)
SEQ_STEP = 16
SLOTS = 3
CHUNK = 128


def tdot(w, act):
    return lax.dot_general(w, act, (((0,), (0,)), ((), ())), preferred_element_type=F32)


def attn_kernel(layer, lens_ref, q_ref, k_ref, v_ref, kc_ref, vc_ref, o_ref, kbuf, vbuf, sems):
    batch, width = q_ref.shape
    dh = kc_ref.shape[3]
    cache_len = kc_ref.shape[4]
    steps = batch // SEQ_STEP

    def copies(step, slot, s):
        b = step * SEQ_STEP + s
        size = (lens_ref[b] + (CHUNK - 1)) // CHUNK * CHUNK
        size = pl.multiple_of(jnp.where(step < SLOTS, cache_len, size), CHUNK)
        span = pl.ds(0, size)
        return [
            pltpu.make_async_copy(c.at[layer, b, :, :, span], buf.at[slot, s, :, :, span], sems.at[slot, n, s])
            for n, (c, buf) in enumerate(((kc_ref, kbuf), (vc_ref, vbuf)))
        ]

    def issue(step, slot):
        for s in range(SEQ_STEP):
            for c in copies(step, slot, s):
                c.start()

    def fetched(step, slot):
        for s in range(SEQ_STEP):
            for c in copies(step, slot, s):
                c.wait()

    for n in range(SLOTS - 1):
        issue(n, n)

    row = lax.broadcasted_iota(jnp.int32, (16, width), 0) % 8
    lane = lax.broadcasted_iota(jnp.int32, (8, width), 1)
    pos = lax.broadcasted_iota(jnp.int32, (16, cache_len), 1)
    row8 = lax.broadcasted_iota(jnp.int32, (8, width), 0)
    first_head = lane < dh

    def body(step, carry):
        slot = lax.rem(step, SLOTS)
        nxt = step + SLOTS - 1

        @pl.when(nxt < steps)
        def _():
            issue(nxt, lax.rem(nxt, SLOTS))

        fetched(step, slot)
        groups = range(SEQ_STEP // 8)
        base = [pl.multiple_of(step * SEQ_STEP + 8 * g, 8) for g in groups]
        q2s, scores = [], []
        for g in groups:
            q8 = q_ref[pl.ds(base[g], 8), :]
            q2 = jnp.concatenate([jnp.where(first_head, q8, 0.0), jnp.where(first_head, 0.0, q8)], axis=0)
            qbd = jnp.concatenate([jnp.where(row == n, q2, 0.0) for n in range(8)], axis=1).astype(BF)
            kb = kbuf[slot, 8 * g:8 * g + 8].reshape(8 * width, cache_len)
            scores.append(jnp.dot(qbd, kb, preferred_element_type=F32))
            q2s.append(q2)
        probs, p_news = [], []
        for g in groups:
            k8 = k_ref[pl.ds(base[g], 8), :]
            k2 = jnp.concatenate([k8, k8], axis=0)
            s_new = jnp.sum(q2s[g] * k2, axis=1, keepdims=True) * (dh ** -0.5)
            lens8 = jnp.zeros((8, width), jnp.int32)
            for n in range(8):
                lens8 = jnp.where(row8 == n, lens_ref[base[g] + n], lens8)
            lens16 = jnp.concatenate([lens8, lens8], axis=0)
            lens_full = jnp.concatenate([lens16] * (cache_len // width), axis=1)
            s = jnp.where(pos < lens_full, scores[g] * (dh ** -0.5), -1e30)
            top = jnp.maximum(jnp.max(s, axis=1, keepdims=True), s_new)
            e = jnp.exp(s - top)
            e_new = jnp.exp(s_new - top)
            inv = 1.0 / (jnp.sum(e, axis=1, keepdims=True) + e_new)
            probs.append((e * inv).astype(BF))
            p_news.append((e_new * inv).astype(BF).astype(F32))
        for g in groups:
            vb = vbuf[slot, 8 * g:8 * g + 8].reshape(8 * width, cache_len)
            mixed = lax.dot_general(probs[g], vb, (((1,), (1,)), ((), ())), preferred_element_type=F32)
            o2 = jnp.zeros((16, width), F32)
            for n in range(8):
                o2 = jnp.where(row == n, mixed[:, n * width:(n + 1) * width], o2)
            v8 = v_ref[pl.ds(base[g], 8), :]
            o2 = o2 + p_news[g] * jnp.concatenate([v8, v8], axis=0)
            o_ref[pl.ds(base[g], 8), :] = jnp.where(first_head, o2[:8], o2[8:])
        return carry

    lax.fori_loop(0, steps, body, 0)


def attention(layer, seq_lens, q, k, v, kc, vc):
    batch, width = q.shape
    heads, dh, cache_len = kc.shape[2:]
    nbytes = kc.shape[1] * heads * dh * cache_len * 2 * 2
    return pl.pallas_call(
        functools.partial(attn_kernel, layer),
        name="attn",
        out_shape=jax.ShapeDtypeStruct((batch, width), F32),
        in_specs=[pl.BlockSpec(memory_space=pltpu.SMEM), VM, VM, VM, ANY, ANY],
        out_specs=VM,
        scratch_shapes=[
            pltpu.VMEM((SLOTS, SEQ_STEP, heads, dh, cache_len), BF),
            pltpu.VMEM((SLOTS, SEQ_STEP, heads, dh, cache_len), BF),
            pltpu.SemaphoreType.DMA((SLOTS, 2, SEQ_STEP)),
        ],
        compiler_params=pltpu.CompilerParams(vmem_limit_bytes=40 * 2**20),
        cost_estimate=pl.CostEstimate(flops=nbytes, bytes_accessed=nbytes, transcendentals=0),
    )(seq_lens, q, k, v, kc, vc)


class Net:
    def __init__(self, send, recv, local):
        self.i = lax.axis_index("x")
        self.j = lax.axis_index("yz")
        self.chip = self.i // 2
        self.core = lax.rem(self.i, 2)
        self.sib = {"x": 2 * self.chip + 1 - self.core}
        self.across = {"x": lax.rem(self.i + 2, 4)}
        self.yother = {"yz": 1 - self.j}
        self.send, self.recv, self.local = send, recv, local
        self.n = 0
        self.m = 0
        self.sent = []

    def greet(self):
        self.barrier = pltpu.get_barrier_semaphore()
        for dx in range(4):
            for dy in range(2):
                if dx or dy:
                    pl.semaphore_signal(self.barrier, inc=1, device_id=self.peer(dx, dy), device_id_type=MESH)

    def met(self):
        pl.semaphore_wait(self.barrier, 7)

    def peer(self, dx, dy):
        return {"x": lax.rem(self.i + dx, 4), "yz": lax.rem(self.j + dy, 2)}

    def put(self, src, dst, to):
        c = pltpu.make_async_remote_copy(
            src_ref=src, dst_ref=dst, send_sem=self.send.at[self.n], recv_sem=self.recv.at[self.n],
            device_id=to, device_id_type=MESH)
        self.n += 1
        c.start()
        self.sent.append(c)
        return c

    def fetch(self, src, dst):
        c = pltpu.make_async_copy(src, dst, self.local.at[self.m])
        self.m += 1
        c.start()
        return c

    def finish(self):
        for c in self.sent:
            c.wait_send()


def norm_send(net, h_own, hx, ssq):
    hf = h_own.astype(F32)
    me = 2 * net.i + net.j
    hx[net.j] = h_own
    ssq[me] = jnp.sum(hf * hf, axis=0, keepdims=True)
    waits = [net.put(hx.at[net.j], hx.at[net.j], net.yother)]
    for dx in range(4):
        for dy in range(2):
            if dx or dy:
                waits.append(net.put(ssq.at[me], ssq.at[me], net.peer(dx, dy)))
    return waits


def norm_finish(waits, hx, ssq, gain, model_dim):
    for c in waits:
        c.wait_recv()
    total = ssq[0]
    for n in range(1, 8):
        total = total + ssq[n]
    inv = lax.rsqrt(total / model_dim + NORM_EPS)
    rows = hx.shape[0] * hx.shape[1]
    hf = hx[...].reshape(rows, hx.shape[2]).astype(F32)
    return (hf * inv * gain).astype(BF)


def slot_of(d):
    return 2 * (d % 2) + d // 2


def rs_first(net, part, got):
    return net.put(part.at[pl.ds(2 * (1 - net.core), 2)], got, net.sib)


def rs_second(net, wait, part, got, out, back):
    wait.wait_recv()
    far = 1 - net.chip
    out[...] = (part[2 * net.core + far].astype(F32) + got[far].astype(F32)).astype(BF)
    return net.put(out, back, net.across)


def rs_last(net, wait, part, got, back):
    mine = part[2 * net.core + net.chip].astype(F32) + got[net.chip].astype(F32)
    wait.wait_recv()
    return mine + back[...].astype(F32)


def qkv_stage(net, xn, ws, bufs, outs, layer_out):
    part, got, out, back = bufs
    first = []
    for n in range(3):
        y = tdot(ws[n][...], xn).astype(BF)
        r = y.shape[0] // 4
        for d in range(4):
            part[n, slot_of(d)] = y[d * r:(d + 1) * r]
        first.append(rs_first(net, part.at[n], got.at[n]))
    second = [rs_second(net, first[n], part.at[n], got.at[n], out.at[n], back.at[n]) for n in range(3)]
    q_out, k_out, v_out, kt_out, vt_out = outs
    for n in range(3):
        y = rs_last(net, second[n], part.at[n], got.at[n], back.at[n]).astype(BF)
        if n:
            (kt_out, vt_out)[n - 1][...] = y
        (q_out, k_out, v_out)[n][...] = y.astype(F32).T


def kernel_a(model_dim, layer, h_ref, g_ref, wq, wk, wv, q_out, k_out, v_out, kt_out, vt_out, ht_out, gx_out,
             hx, ssq, gx, w_buf, part, got, out, back, send, recv, local):
    net = Net(send, recv, local)
    net.greet()
    loads = [net.fetch(w.at[layer], w_buf.at[n]) for n, w in enumerate((wq, wk, wv))]
    h_own = h_ref[...].astype(F32).T.astype(BF)
    ht_out[...] = h_own
    gx[net.j] = g_ref[...]
    net.met()
    waits = norm_send(net, h_own, hx, ssq)
    waits.append(net.put(gx.at[net.j], gx.at[net.j], net.yother))
    for c in loads:
        c.wait()
    waits[-1].wait_recv()
    gains = gx[...].reshape(2 * gx.shape[1], gx.shape[2])
    gx_out[...] = gains
    xn = norm_finish(waits[:-1], hx, ssq, gains[:, layer:layer + 1], model_dim)
    qkv_stage(net, xn, [w_buf.at[n] for n in range(3)], (part, got, out, back),
              (q_out, k_out, v_out, kt_out, vt_out), layer)
    net.finish()


def gather_x(net, buf):
    me = buf.at[net.i]
    across = net.put(me, me, net.across)
    sib = net.put(me, me, net.sib)
    return sib, across


def gather_forward(net, buf, across):
    across.wait_recv()
    far = buf.at[lax.rem(net.i + 2, 4)]
    return net.put(far, far, net.sib)


def sum_yz(net, y, part, got):
    r = y.shape[0] // 2
    part[0] = y[:r].astype(BF)
    part[1] = y[r:].astype(BF)
    c = net.put(part.at[1 - net.j], got, net.yother)
    c.wait_recv()
    return part[net.j].astype(F32) + got[...].astype(F32)


def post_attention(net, model_dim, o_ref, h_own, gain, wo, win, wout, s, wait_w):
    s["o"][net.i] = o_ref[...].T.astype(BF)
    net.met()
    sib, across = gather_x(net, s["o"])
    wait_w("wo")
    fwd = gather_forward(net, s["o"], across)
    sib.wait_recv()
    fwd.wait_recv()
    o_all = s["o"][...].reshape(-1, s["o"].shape[2])
    h1 = (h_own.astype(F32) + sum_yz(net, tdot(wo[...], o_all), s["ypart1"], s["ygot1"])).astype(BF)
    waits = norm_send(net, h1, s["hx1"], s["ssq1"])
    wait_w("win")
    xn = norm_finish(waits, s["hx1"], s["ssq1"], gain, model_dim)
    r = win.shape[1] // 4
    y = tdot(win[...], xn).astype(BF)
    for d in range(4):
        s["upart"][slot_of(d)] = y[d * r:(d + 1) * r]
    first = rs_first(net, s["upart"], s["ugot"])
    second = rs_second(net, first, s["upart"], s["ugot"], s["uout"], s["uback"])
    up = rs_last(net, second, s["upart"], s["ugot"], s["uback"]).astype(BF)
    s["u"][net.i] = jax.nn.gelu(up.astype(F32)).astype(BF)
    sib, across = gather_x(net, s["u"])
    wait_w("wout")
    fwd = gather_forward(net, s["u"], across)
    sib.wait_recv()
    fwd.wait_recv()
    u_all = s["u"][...].reshape(-1, s["u"].shape[2])
    return (h1.astype(F32) + sum_yz(net, tdot(wout[...], u_all), s["ypart2"], s["ygot2"])).astype(BF)


POST = ("o", "ypart1", "ygot1", "hx1", "ssq1", "upart", "ugot", "uout", "uback", "u", "ypart2", "ygot2", "hx2", "ssq2",
        "wo", "win", "wout")


def post_shapes(blk, batch, f_loc, k_o):
    r = f_loc // 4
    return [
        pltpu.VMEM((4, blk, batch), BF),
        pltpu.VMEM((2, blk, batch), BF), pltpu.VMEM((blk, batch), BF),
        pltpu.VMEM((2, blk, batch), BF), pltpu.VMEM((8, 1, batch), F32),
        pltpu.VMEM((4, r, batch), BF), pltpu.VMEM((2, r, batch), BF), pltpu.VMEM((r, batch), BF), pltpu.VMEM((r, batch), BF),
        pltpu.VMEM((4, r, batch), BF),
        pltpu.VMEM((2, blk, batch), BF), pltpu.VMEM((blk, batch), BF),
        pltpu.VMEM((2, blk, batch), BF), pltpu.VMEM((8, 1, batch), F32),
        pltpu.VMEM((k_o, 2 * blk), BF), pltpu.VMEM((2 * blk, f_loc), BF), pltpu.VMEM((f_loc, 2 * blk), BF),
    ]


def kernel_b(model_dim, layers, layer, o_ref, ht_ref, gx_ref, wo, win, wout, wq, wk, wv,
             q_out, k_out, v_out, kt_out, vt_out, ht_out, *rest):
    s = dict(zip(POST, rest))
    w_buf, part, got, out, back, send, recv, local = rest[len(POST):]
    net = Net(send, recv, local)
    net.greet()
    loads = {n: net.fetch(w.at[layer], s[n]) for n, w in (("wo", wo), ("win", win), ("wout", wout))}
    qkv_loads = [net.fetch(w.at[layer + 1], w_buf.at[n]) for n, w in enumerate((wq, wk, wv))]
    gains = gx_ref[...]
    h2 = post_attention(net, model_dim, o_ref, ht_ref[...], gains[:, layers + layer:layers + layer + 1],
                        s["wo"], s["win"], s["wout"], s, lambda n: loads[n].wait())
    ht_out[...] = h2
    waits = norm_send(net, h2, s["hx2"], s["ssq2"])
    for c in qkv_loads:
        c.wait()
    xn = norm_finish(waits, s["hx2"], s["ssq2"], gains[:, layer + 1:layer + 2], model_dim)
    qkv_stage(net, xn, [w_buf.at[n] for n in range(3)], (part, got, out, back),
              (q_out, k_out, v_out, kt_out, vt_out), layer + 1)
    net.finish()


def kernel_c(model_dim, layers, layer, o_ref, ht_ref, gx_ref, wo, win, wout, wu, h_out, logit_out, *rest):
    s = dict(zip(POST, rest))
    w_buf, send_a, got_a, send_b, got_b, stage, send, recv, local = rest[len(POST):]
    net = Net(send, recv, local)
    net.greet()
    loads = {n: net.fetch(w.at[layer], s[n]) for n, w in (("wo", wo), ("win", win), ("wout", wout))}
    wu_load = net.fetch(wu, w_buf)
    gains = gx_ref[...]
    h2 = post_attention(net, model_dim, o_ref, ht_ref[...], gains[:, layers + layer:layers + layer + 1],
                        s["wo"], s["win"], s["wout"], s, lambda n: loads[n].wait())
    waits = norm_send(net, h2, s["hx2"], s["ssq2"])
    h_out[...] = h2.astype(F32).T.astype(BF)
    wu_load.wait()
    xn = norm_finish(waits, s["hx2"], s["ssq2"], gains[:, 2 * layers:2 * layers + 1], model_dim)
    v_loc = got_b.shape[0]
    step = 512
    spans = [(a, min(step, v_loc - a)) for a in range(0, v_loc, step)]

    def product(chip, core, a, n):
        start = pl.multiple_of((2 * chip + core) * v_loc + a, 16)
        return jnp.dot(w_buf[pl.ds(start, n), :], xn, preferred_element_type=F32)

    first, second = [], []

    def stage1(a, n):
        for chip in range(2):
            send_a[chip, pl.ds(a, n)] = product(chip, 1 - net.core, a, n).astype(BF)
        first.append(net.put(send_a.at[:, pl.ds(a, n)], got_a.at[:, pl.ds(a, n)], net.sib))

    def stage2(r, a, n):
        far = 1 - net.chip
        y = product(far, net.core, a, n)
        first[r].wait_recv()
        send_b[pl.ds(a, n)] = (y + got_a[far, pl.ds(a, n)].astype(F32)).astype(BF)
        second.append(net.put(send_b.at[pl.ds(a, n)], got_b.at[pl.ds(a, n)], net.across))

    stage1(*spans[0])
    for r in range(len(spans)):
        if r + 1 < len(spans):
            stage1(*spans[r + 1])
        stage2(r, *spans[r])
    stores = []
    for r, (a, n) in enumerate(spans):
        y = product(net.chip, net.core, a, n) + got_a[net.chip, pl.ds(a, n)].astype(F32)
        second[r].wait_recv()
        stage[pl.ds(a, n)] = y + got_b[pl.ds(a, n)].astype(F32)
        stores.append(net.fetch(stage.at[pl.ds(a, n)], logit_out.at[pl.ds(a, n)]))
    for c in stores:
        c.wait()
    net.finish()


def sds(shape, dtype):
    return jax.ShapeDtypeStruct(shape, dtype)


def solution(mesh):
    def decode_step(h_loc, seq_lens, k_cache, v_cache, g_attn, w_q, w_k, w_v, w_o, g_mlp, w_in, w_out, g_final, w_unemb):
        batch, blk = h_loc.shape
        layers = w_q.shape[0]
        model_dim = 8 * blk
        heads, dh = k_cache.shape[2], k_cache.shape[4]
        k_in, n_qkv = w_q.shape[1:]
        f_loc = w_in.shape[2]
        v_all = w_unemb.shape[1]
        v_loc = v_all // 4
        width = heads * dh
        kc = jnp.swapaxes(k_cache, 3, 4)
        vc = jnp.swapaxes(v_cache, 3, 4)
        wu = w_unemb.T
        gains = jnp.concatenate([g_attn, g_mlp, g_final[None]], axis=0)
        gains = jnp.pad(gains, ((0, 128 - gains.shape[0]), (0, 0))).T.astype(F32)

        qkv_bufs = [
            pltpu.VMEM((3, k_in, n_qkv), BF),
            pltpu.VMEM((3, 4, width, batch), BF), pltpu.VMEM((3, 2, width, batch), BF),
            pltpu.VMEM((3, width, batch), BF), pltpu.VMEM((3, width, batch), BF),
        ]
        qkv_outs = [sds((batch, width), F32)] * 3 + [sds((width, batch), BF)] * 2 + [sds((blk, batch), BF)]

        def sems(remote, local):
            return [pltpu.SemaphoreType.DMA((remote,)), pltpu.SemaphoreType.DMA((remote,)), pltpu.SemaphoreType.DMA((local,))]

        def params(cid):
            return pltpu.CompilerParams(collective_id=cid, has_side_effects=True, vmem_limit_bytes=56 * 2**20)

        q, k, v, kt, vt, ht, gx = pl.pallas_call(
            functools.partial(kernel_a, model_dim, 0),
            name="stage_a",
            out_shape=qkv_outs + [sds((2 * blk, 128), F32)],
            in_specs=[VM, VM, ANY, ANY, ANY],
            out_specs=[VM] * 7,
            scratch_shapes=[pltpu.VMEM((2, blk, batch), BF), pltpu.VMEM((8, 1, batch), F32),
                            pltpu.VMEM((2, blk, 128), F32)] + qkv_bufs + sems(15, 3),
            compiler_params=params(0),
        )(h_loc, gains, w_q, w_k, w_v)
        kts, vts = [kt], [vt]
        for layer in range(layers - 1):
            o = attention(layer, seq_lens, q, k, v, kc, vc)
            q, k, v, kt, vt, ht = pl.pallas_call(
                functools.partial(kernel_b, model_dim, layers, layer),
                name="stage_b",
                out_shape=qkv_outs,
                in_specs=[VM, VM, VM] + [ANY] * 6,
                out_specs=[VM] * 6,
                scratch_shapes=post_shapes(blk, batch, f_loc, w_o.shape[1]) + qkv_bufs + sems(32, 6),
                compiler_params=params(1 + layer),
            )(o, ht, gx, w_o, w_in, w_out, w_q, w_k, w_v)
            kts.append(kt)
            vts.append(vt)
        layer = layers - 1
        o = attention(layer, seq_lens, q, k, v, kc, vc)
        h_out, logits_t = pl.pallas_call(
            functools.partial(kernel_c, model_dim, layers, layer),
            name="stage_c",
            out_shape=[sds((batch, blk), BF), sds((v_loc, batch), F32)],
            in_specs=[VM, VM, VM] + [ANY] * 4,
            out_specs=[VM, ANY],
            scratch_shapes=post_shapes(blk, batch, f_loc, w_o.shape[1]) + [
                pltpu.VMEM((v_all, 2 * blk), BF),
                pltpu.VMEM((2, v_loc, batch), BF), pltpu.VMEM((2, v_loc, batch), BF),
                pltpu.VMEM((v_loc, batch), BF), pltpu.VMEM((v_loc, batch), BF), pltpu.VMEM((v_loc, batch), F32),
            ] + sems(64, 16),
            compiler_params=params(layers),
        )(o, ht, gx, w_o, w_in, w_out, wu)

        def entries(parts):
            return jnp.transpose(jnp.stack(parts).reshape(layers, heads, dh, batch), (0, 3, 1, 2))

        return h_out, logits_t.T, entries(kts), entries(vts)

    emb_spec = P('dp', ('x', 'yz'))
    gain_spec = P(None, ('x', 'yz'))
    cache_spec = P(None, 'dp', ('yz', 'x'), None, None)
    in_rows = P(None, 'x', 'yz')
    out_rows = P(None, 'yz', 'x')
    new_spec = P(None, 'dp', ('yz', 'x'), None)
    in_specs = (emb_spec, P('dp'), cache_spec, cache_spec, gain_spec, in_rows, in_rows, in_rows, out_rows, gain_spec, in_rows, out_rows, P(('x', 'yz')), P('x', 'yz'))
    out_specs = (emb_spec, P('dp', ('yz', 'x')), new_spec, new_spec)
    return jax.shard_map(decode_step, mesh=mesh, in_specs=in_specs, out_specs=out_specs, check_vma=False)
```

time: 467 us -> 216 us (0.46)
  Pallas kernels: 0 us -> 199 us
  blocking collectives: 178 us -> 0 us
  waiting for transfers between devices: 165 us -> 0 us
  matrix products: 75 us -> 0 us
  other arithmetic: 17.6 us -> 2.06 us
  between operations: 14.3 us -> 0.73 us
    pallas_call x0 -> x5, Pallas kernels: none -> 199 us  [the longest x1 85.8 us: decode_step(): pl.pallas_call(functools.partial(kernel_c, model_dim, layers, layer), nam...]
    psum x5 -> x0, blocking collectives: 114 us -> none  [norm_shard(): lax.psum(jnp.sum(h_f32 * h_f32, axis=-1, keepdims=True), group_axes)]
    reduce_scatter x3 -> x0, waiting for transfers between devices: 101 us -> none  [the longest x1 63.6 us: decode_step(): lax.psum_scatter(matmul_bf16(row_block, w_unemb), 'x', scatter_dimension=...]
    dot_general x17 -> x0, matrix products: 75 us -> none  [the longest x2 28.2 us: attend(): jnp.einsum('bhs,bhsd->bhd', p_cache, v_cache, preferred_element_type=jnp....]
    unnamed x23 -> x0, waiting for transfers between devices: 63.9 us -> none
    all_gather x9 -> x0, blocking collectives: 63.4 us -> none  [the longest x5 26.2 us: decode_step(): row_block = lax.all_gather(normed, 'yz', axis=1, tiled=True)]
    convert_element_type x15 -> x1, other arithmetic: 9.81 us -> 0.64 us  [decode_step(): gains = jnp.pad(gains, ((0, 128 - gains.shape[0]), (0, 0))).T.astype(F32)]
    unnamed x42 -> x30, local copies, waits for them, and re-layouts: 12.8 us -> 13.3 us
  transfers between devices with their start and end apart: 13 -> 0, of which waited for: 13 -> 0; matrix products, arithmetic and copies ran while one was open for 15% -> 0% of each run, Pallas kernels for 0% -> 0%
where the time goes in v1:
time: 216 us; the launch traced here: 215 us
  Pallas kernels  199 us (92%)
  local copies, waits for them, and re-layouts  13.4 us (6%)
    pallas_call x1, Pallas kernels, decode_step(): pl.pallas_call(functools.partial(kernel_c, model_dim, layers, layer), nam...  85.8 us
    pallas_call x2, Pallas kernels, attention(): pl.pallas_call(functools.partial(attn_kernel, layer), name='attn', out_sh...  49.5 us
    pallas_call x1, Pallas kernels, decode_step(): pl.pallas_call(functools.partial(kernel_b, model_dim, layers, layer), nam...  45.7 us
    pallas_call x1, Pallas kernels, decode_step(): pl.pallas_call(functools.partial(kernel_a, model_dim, 0), name='stage_a',...  18.2 us
    unnamed x30, local copies, waits for them, and re-layouts  13.3 us

profile of v1, /device:TPU:0, one launch (start us, length us, event | category | flops | bytes accessed | tf_op | source)
XLA Modules:
  0.0 215.4 jit_solution(7287255710637664831)
XLA Ops:
  0.6 0.7 pad_maximum_fusion
  1.3 0.1 copy.21
  1.5 0.6 convert_bitcast_fusion.g_ref
  2.1 18.2 %stage_a.1 = (f32[256,128]{1,0:T(8,128)}, f32[256,128]{1,0:T(8,128)}, f32[256,128]{1,0:T(8,128)}, bf16[128,256]{1,0:T(8,128)(2,1)}, bf16[128,256]{1,0:T(8,128)(2...) custom-call(bf16[256,128]{1,0:T(8,128)(2,1)} %h_ref.1, f32[128,128]{1,0:T(8,128)} %convert_bitcast_fusion.g_ref, ...), custom_call_target="tpu_custom_call" | custom-call | tf_op jit(solution)/shard_map/stage_a/pallas_call | solution.py:440
  20.3 0.0 copy-start.2
  20.3 0.9 copy-done.2
  21.2 0.0 copy-start.3
  21.2 0.9 copy-done.3
  22.1 0.0 copy-start.4
  22.1 0.9 copy-done.4
  23.0 0.0 copy-start.8
  23.0 0.7 copy-done.8
  23.7 24.7 %attn.2.o_ref = f32[256,128]{1,0:T(8,128)S(1)} custom-call(s32[256]{0:T(256)S(1)} %copy-done.8, f32[256,128]{1,0:T(8,128)S(1)} %copy-done.2, f32[256,128]{1,0:T(8,128)S(1)} %copy-done.3, f32[256,128]{1,0:T(8,128)S(1)} %copy-done.4, bf16[2,256,2,64,512]{4,3,2,1,0:T(8,128)(2,1)} %bitcast.2.kc_ref, bf16[2,256,2,64,512]{4,3,2,1,0:T(8,128)(2,1)} %bitcast.3.vc_ref), custom_call_target="tpu_custom_call" | custom-call | flops 67108864 | bytes 67108864 | tf_op jit(solution)/shard_map/attn/pallas_call | solution.py:114
  48.4 0.0 copy-start.1
  48.4 0.6 copy-done.1
  49.1 0.0 copy-start.9
  49.1 45.7 %stage_b.1 = (f32[256,128]{1,0:T(8,128)}, f32[256,128]{1,0:T(8,128)}, f32[256,128]{1,0:T(8,128)}, bf16[128,256]{1,0:T(8,128)(2,1)}, bf16[128,256]{1,0:T(8,128)(2,1)}, /*index=5*/bf16[128,256]{1,0:T(8,128)(2,1)}) custom-call(f32[256,128]{1,0:T(8,128)} %copy-done.1, bf16[128,256]{1,0:T(8,128)(2,1)} %get-tuple-element.22.ht_ref, ...), custom_call_target="tpu_custom_call" | custom-call | tf_op jit(solution)/shard_map/stage_b/pallas_call | solution.py:453
  94.7 0.0 copy-done.9
  94.7 0.0 copy-start.5
  94.8 0.9 copy-done.5
  95.6 0.0 copy-start.6
  95.7 0.9 copy-done.6
  96.6 0.0 copy-start.7
  96.6 0.9 copy-done.7
  97.5 0.0 copy-start.10
  97.5 0.0 copy-start.11
  97.5 0.0 copy-start.12
  97.5 0.0 copy-start.13
  97.5 24.8 %attn.3.o_ref = f32[256,128]{1,0:T(8,128)S(1)} custom-call(s32[256]{0:T(256)S(1)} %copy-done.9, f32[256,128]{1,0:T(8,128)S(1)} %copy-done.5, f32[256,128]{1,0:T(8,128)S(1)} %copy-done.6, f32[256,128]{1,0:T(8,128)S(1)} %copy-done.7, bf16[2,256,2,64,512]{4,3,2,1,0:T(8,128)(2,1)} %bitcast.2.kc_ref, bf16[2,256,2,64,512]{4,3,2,1,0:T(8,128)(2,1)} %bitcast.3.vc_ref), custom_call_target="tpu_custom_call" | custom-call | flops 67108864 | bytes 67108864 | tf_op jit(solution)/shard_map/attn/pallas_call | solution.py:114
  122.3 0.0 copy-start
  122.3 0.6 copy-done
  122.9 0.0 copy-done.10
  122.9 0.0 copy-done.11
  122.9 0.0 copy-done.12
  122.9 0.0 copy-done.13
  122.9 0.7 maximum_bitcast_fusion
  123.7 85.8 %stage_c.1 = (bf16[256,128]{1,0:T(8,128)(2,1)}, f32[4016,256]{1,0:T(8,128)}) custom-call(f32[256,128]{1,0:T(8,128)} %copy-done, bf16[128,256]{1,0:T(8,128)(2,1)} %get-tuple-element.27.ht_ref, f32[256,128]{1,0:T(8,128)} %get-tuple-element.23.gx_ref, bf16[2,512,256]{2,1,0:T(8,128)(2,1)} %wo.3, bf16[2,256,1408]{2,1,0:T(8,128)(2,1)} %win.3, ...), custom_call_target="tpu_custom_call" | custom-call | tf_op jit(solution)/shard_map/stage_c/pallas_call | solution.py:466
  209.5 1.5 copy.24
  211.0 4.4 %copy.25 = f32[256,4016]{0,1:T(8,128)} copy(f32[256,4016]{0,1:T(8,128)} %bitcast.16) | data formatting | bytes 8224768
Async XLA Ops:
  20.3 0.9 copy-start.2
  21.2 0.9 copy-start.3
  22.1 0.9 copy-start.4
  23.0 0.7 copy-start.8
  48.4 0.7 copy-start.1
  49.1 45.7 %copy-start.9 = (s32[256]{0:T(256)S(1)}, s32[256]{0:T(256)}, u32[]{:S(2)}) copy-start(s32[256]{0:T(256)} %lens_ref.3) | copy-start | bytes 3076
  94.7 0.9 copy-start.5
  95.6 0.9 copy-start.6
  96.6 0.9 copy-start.7
  97.5 25.5 %copy-start.10 = (bf16[128,256]{1,0:T(8,128)(2,1)S(1)}, bf16[128,256]{1,0:T(8,128)(2,1)}, u32[]{:S(2)}) copy-start(bf16[128,256]{1,0:T(8,128)(2,1)} %get-tuple-element.30) | copy-start | bytes 196612
  97.5 25.5 %copy-start.11 = (bf16[128,256]{1,0:T(8,128)(2,1)S(1)}, bf16[128,256]{1,0:T(8,128)(2,1)}, u32[]{:S(2)}) copy-start(bf16[128,256]{1,0:T(8,128)(2,1)} %get-tuple-element.32) | copy-start | bytes 196612
  97.5 25.5 %copy-start.12 = (bf16[128,256]{1,0:T(8,128)(2,1)S(1)}, bf16[128,256]{1,0:T(8,128)(2,1)}, u32[]{:S(2)}) copy-start(bf16[128,256]{1,0:T(8,128)(2,1)} %get-tuple-element.31) | copy-start | bytes 196612
  97.5 25.5 %copy-start.13 = (bf16[128,256]{1,0:T(8,128)(2,1)S(1)}, bf16[128,256]{1,0:T(8,128)(2,1)}, u32[]{:S(2)}) copy-start(bf16[128,256]{1,0:T(8,128)(2,1)} %get-tuple-element.33) | copy-start | bytes 196612
  122.3 0.7 copy-start

commit v2 on v0

v2 whole, which is shorter than its diff:
```python
import functools

import jax
import jax.numpy as jnp
from jax import lax
from jax.experimental import pallas as pl
from jax.experimental.pallas import tpu as pltpu
from jax.sharding import PartitionSpec as P

NORM_EPS = 1e-6
MESH = pl.DeviceIdType.MESH
BF = jnp.bfloat16
F32 = jnp.float32
ANY = pl.BlockSpec(memory_space=pl.ANY)
VM = pl.BlockSpec(memory_space=pltpu.VMEM)
SEQ_STEP = 16
SLOTS = 5
WINDOWS = (768, 176, 208, 224, 240, 768, 176, 208, 224)
COPIES = 150


def tdot(w, act):
    return lax.dot_general(w, act, (((0,), (0,)), ((), ())), preferred_element_type=F32)


class Attention:
    def __init__(self, lens_ref, kc_ref, vc_ref, q_ref, k_ref, v_ref, o_ref, kbuf, vbuf, pbuf, pnew, sems):
        self.lens, self.kc, self.vc = lens_ref, kc_ref, vc_ref
        self.q, self.k, self.v, self.o = q_ref, k_ref, v_ref, o_ref
        self.kbuf, self.vbuf, self.pbuf, self.pnew, self.sems = kbuf, vbuf, pbuf, pnew, sems
        self.layers = kc_ref.shape[0]
        self.batch, self.width = q_ref.shape
        self.dh, self.cache_len = kc_ref.shape[3], kc_ref.shape[4]
        self.steps = self.batch // SEQ_STEP
        self.groups = range(SEQ_STEP // 8)
        self.row = lax.broadcasted_iota(jnp.int32, (16, self.width), 0) % 8
        self.pos = lax.broadcasted_iota(jnp.int32, (16, self.cache_len), 1)
        self.row8 = lax.broadcasted_iota(jnp.int32, (8, self.width), 0)
        self.first_head = lax.broadcasted_iota(jnp.int32, (8, self.width), 1) < self.dh

    def copy(self, g, n):
        slot = lax.rem(g, SLOTS)
        src, buf = ((self.kc, self.kbuf), (self.vc, self.vbuf))[n]
        block = src.at[g // self.steps, pl.ds(lax.rem(g, self.steps) * SEQ_STEP, SEQ_STEP)]
        return pltpu.make_async_copy(block, buf.at[slot], self.sems.at[slot, n])

    def issue(self, g):
        for n in range(2):
            self.copy(g, n).start()

    def start(self):
        for g in range(SLOTS):
            self.issue(jnp.int32(g))

    def base(self, step, g):
        return pl.multiple_of(step * SEQ_STEP + 8 * g, 8)

    def score(self, step, slot):
        q2s, scores = [], []
        for g in self.groups:
            q8 = self.q[pl.ds(self.base(step, g), 8), :]
            q2 = jnp.concatenate([jnp.where(self.first_head, q8, 0.0), jnp.where(self.first_head, 0.0, q8)], axis=0)
            qbd = jnp.concatenate([jnp.where(self.row == n, q2, 0.0) for n in range(8)], axis=1).astype(BF)
            kb = self.kbuf[slot, 8 * g:8 * g + 8].reshape(8 * self.width, self.cache_len)
            scores.append(jnp.dot(qbd, kb, preferred_element_type=F32))
            q2s.append(q2)
        return q2s, scores

    def softmax(self, step, q2s, scores):
        for g in self.groups:
            k8 = self.k[pl.ds(self.base(step, g), 8), :]
            k2 = jnp.concatenate([k8, k8], axis=0)
            s_new = jnp.sum(q2s[g] * k2, axis=1, keepdims=True) * (self.dh ** -0.5)
            lens8 = jnp.zeros((8, self.width), jnp.int32)
            for n in range(8):
                lens8 = jnp.where(self.row8 == n, self.lens[self.base(step, g) + n], lens8)
            lens16 = jnp.concatenate([lens8, lens8], axis=0)
            lens_full = jnp.concatenate([lens16] * (self.cache_len // self.width), axis=1)
            s = jnp.where(self.pos < lens_full, scores[g] * (self.dh ** -0.5), -1e30)
            top = jnp.maximum(jnp.max(s, axis=1, keepdims=True), s_new)
            e = jnp.exp(s - top)
            e_new = jnp.exp(s_new - top)
            inv = 1.0 / (jnp.sum(e, axis=1, keepdims=True) + e_new)
            self.pbuf[g] = (e * inv).astype(BF)
            self.pnew[g] = jnp.broadcast_to((e_new * inv).astype(BF).astype(F32), (16, self.width))

    def mix(self, step, slot):
        w = self.width
        for g in self.groups:
            vb = self.vbuf[slot, 8 * g:8 * g + 8].reshape(8 * w, self.cache_len)
            mixed = lax.dot_general(self.pbuf[g], vb, (((1,), (1,)), ((), ())), preferred_element_type=F32)
            o2 = jnp.zeros((16, w), F32)
            for n in range(8):
                o2 = jnp.where(self.row == n, mixed[:, n * w:(n + 1) * w], o2)
            v8 = self.v[pl.ds(self.base(step, g), 8), :]
            o2 = o2 + self.pnew[g] * jnp.concatenate([v8, v8], axis=0)
            self.o[pl.ds(self.base(step, g), 8), :] = jnp.where(self.first_head, o2[:8], o2[8:])

    def layer(self, layer):
        first = layer * self.steps
        last = self.layers * self.steps

        def fetched(step, n):
            self.copy(first + step, n).wait()
            return lax.rem(first + step, SLOTS)

        self.softmax(0, *self.score(0, fetched(jnp.int32(0), 0)))

        def body(step, carry):
            nxt = first + step - 2 + SLOTS

            @pl.when((step >= 2) & (nxt < last))
            def _():
                self.issue(nxt)

            k_slot = fetched(step, 0)
            v_slot = fetched(step - 1, 1)
            q2s, scores = self.score(step, k_slot)
            self.mix(step - 1, v_slot)
            self.softmax(step, q2s, scores)
            return carry

        lax.fori_loop(1, self.steps, body, 0)
        self.mix(self.steps - 1, fetched(jnp.int32(self.steps - 1), 1))
        for g in (first + self.steps - 2 + SLOTS, first + self.steps - 1 + SLOTS):
            if g < last:
                self.issue(jnp.int32(g))


class Net:
    def __init__(self, send, recv, local):
        self.i = lax.axis_index("x")
        self.j = lax.axis_index("yz")
        self.chip = self.i // 2
        self.core = lax.rem(self.i, 2)
        self.sib = {"x": 2 * self.chip + 1 - self.core}
        self.across = {"x": lax.rem(self.i + 2, 4)}
        self.yother = {"yz": 1 - self.j}
        self.send, self.recv, self.local = send, recv, local
        self.n = 0
        self.m = 0
        self.sent = []

    def greet(self):
        self.barrier = pltpu.get_barrier_semaphore()
        for dx in range(4):
            for dy in range(2):
                if dx or dy:
                    pl.semaphore_signal(self.barrier, inc=1, device_id=self.peer(dx, dy), device_id_type=MESH)

    def met(self):
        pl.semaphore_wait(self.barrier, 7)

    def peer(self, dx, dy):
        return {"x": lax.rem(self.i + dx, 4), "yz": lax.rem(self.j + dy, 2)}

    def put(self, src, dst, to):
        c = pltpu.make_async_remote_copy(
            src_ref=src, dst_ref=dst, send_sem=self.send.at[self.n], recv_sem=self.recv.at[self.n],
            device_id=to, device_id_type=MESH)
        self.n += 1
        c.start()
        self.sent.append(c)
        return c

    def fetch(self, src, dst):
        c = pltpu.make_async_copy(src, dst, self.local.at[self.m])
        self.m += 1
        c.start()
        return c

    def finish(self):
        for c in self.sent:
            c.wait_send()


def slot_of(d):
    return 2 * (d % 2) + d // 2


def rs_first(net, part, got):
    return net.put(part.at[pl.ds(2 * (1 - net.core), 2)], got, net.sib)


def rs_second(net, wait, part, got, out, back):
    wait.wait_recv()
    far = 1 - net.chip
    out[...] = (part[2 * net.core + far].astype(F32) + got[far].astype(F32)).astype(BF)
    return net.put(out, back, net.across)


def rs_last(net, wait, part, got, back):
    mine = part[2 * net.core + net.chip].astype(F32) + got[net.chip].astype(F32)
    wait.wait_recv()
    return mine + back[...].astype(F32)


def qkv_stage(net, xn, w, s, q_out, k_out, v_out, kt_out, vt_out):
    part, got, out, back = s["qkv_part"], s["qkv_got"], s["qkv_out"], s["qkv_back"]
    first = []
    for n in range(3):
        y = tdot(w[n], xn).astype(BF)
        r = y.shape[0] // 4
        for d in range(4):
            part[n, slot_of(d)] = y[d * r:(d + 1) * r]
        first.append(rs_first(net, part.at[n], got.at[n]))
    second = [rs_second(net, first[n], part.at[n], got.at[n], out.at[n], back.at[n]) for n in range(3)]
    for n in range(3):
        y = rs_last(net, second[n], part.at[n], got.at[n], back.at[n]).astype(BF)
        if n:
            (kt_out, vt_out)[n - 1][...] = y
        (q_out, k_out, v_out)[n][...] = y.astype(F32).T


def gather_x(net, buf):
    me = buf.at[net.i]
    across = net.put(me, me, net.across)
    sib = net.put(me, me, net.sib)
    return sib, across


def gather_forward(net, buf, across):
    across.wait_recv()
    far = buf.at[lax.rem(net.i + 2, 4)]
    return net.put(far, far, net.sib)


def sum_yz(net, y, part, got):
    r = y.shape[0] // 2
    part[0] = y[:r].astype(BF)
    part[1] = y[r:].astype(BF)
    c = net.put(part.at[1 - net.j], got, net.yother)
    c.wait_recv()
    return part[net.j].astype(F32) + got[...].astype(F32)


def norm_send(net, h_own, hx, ssq, far=False):
    hf = h_own.astype(F32)
    me = 2 * net.i + net.j
    hx[0, net.j] = h_own
    ssq[me] = jnp.sum(hf * hf, axis=0, keepdims=True)
    mine = hx.at[0, net.j]
    stats = []
    for dx in range(4):
        for dy in range(2):
            if dx or dy:
                stats.append(net.put(ssq.at[me], ssq.at[me], net.peer(dx, dy)))
    near = net.put(mine, hx.at[0, net.j], net.yother)
    fars = [net.put(mine, hx.at[1, net.j], to) for to in (net.across, net.peer(2, 1))] if far else []
    return stats, near, fars


def norm_scale(stats, ssq, model_dim):
    for c in stats:
        c.wait_recv()
    total = ssq[0]
    for n in range(1, 8):
        total = total + ssq[n]
    return lax.rsqrt(total / model_dim + NORM_EPS)


def normed(hx, inv, gain):
    rows = hx.shape[0] * hx.shape[1]
    return (hx[...].reshape(rows, hx.shape[2]).astype(F32) * inv * gain).astype(BF)


def columns(gx, n):
    return jnp.concatenate([gx[0].T[:, n:n + 1], gx[1].T[:, n:n + 1]], axis=0)


def kernel(names, model_dim, h_ref, lens_ref, kc, vc, g_ref, wq, wk, wv, wo, win, wout, wu, h_out, logit_out, kt_out, vt_out, *rest):
    s = dict(zip(names, rest))
    kv_sems, send, recv, local = rest[len(names):]
    layers = wq.shape[0]
    net = Net(send, recv, local)
    net.greet()
    mats = (("wo", wo), ("win", win), ("wout", wout))
    loads = {("qkv", 0): [net.fetch(w.at[0], s["wqkv0"].at[n]) for n, w in enumerate((wq, wk, wv))]}
    att = Attention(lens_ref, kc, vc, s["q"], s["k"], s["v"], s["att"], s["kbuf"], s["vbuf"], s["pbuf"], s["pnew"], kv_sems)
    for l in range(layers):
        if l:
            loads["qkv", l] = [net.fetch(w.at[l], s[f"wqkv{l}"].at[n]) for n, w in enumerate((wq, wk, wv))]
        for name, w in mats:
            loads[name, l] = [net.fetch(w.at[l], s[f"{name}{l}"])]
    att.start()

    def weight(name, l):
        for c in loads.pop((name, l)):
            c.wait()
        return s[f"{name}{l}"]

    v_loc = logit_out.shape[0]
    early = []
    far_chip = 1 - net.chip

    def window(n):
        a = sum(WINDOWS[:n])
        for core in range(2):
            src = wu.at[pl.ds(pl.multiple_of((2 * far_chip + core) * v_loc + a, 16), WINDOWS[n])]
            early.append(net.put(src, s["wm"].at[core, pl.ds(a, WINDOWS[n])], net.across))

    gx, gfar = s["gx"], s["gfar"]
    h_own = h_ref[...].astype(F32).T.astype(BF)
    gx[net.j] = g_ref[...]
    net.met()
    g_near = net.put(gx.at[net.j], gx.at[net.j], net.yother)
    stats, near, _ = norm_send(net, h_own, s["hx_a0"], s["ssq_a0"])
    g_fars = [net.put(gx.at[net.j], gfar.at[net.j], to) for to in (net.across, net.peer(2, 1))]
    g_near.wait_recv()
    wn = 0
    for l in range(layers):
        inv = norm_scale(stats, s[f"ssq_a{l}"], model_dim)
        near.wait_recv()
        xn = normed(s[f"hx_a{l}"].at[0], inv, columns(gx, l))
        sl = {k[:-1]: s[k] for k in s if k.endswith(str(l))}
        qkv_stage(net, xn, wait_qkv(loads, s, l), sl, s["q"], s["k"], s["v"], kt_out.at[l], vt_out.at[l])
        window(wn)
        wn += 1
        att.layer(l)
        if l == layers - 1:
            wu_load = net.fetch(wu, s["wu"])
        o = sl["o"]
        o[net.i] = s["att"][...].T.astype(BF)
        sib, across = gather_x(net, o)
        w = weight("wo", l)
        fwd = gather_forward(net, o, across)
        window(wn)
        wn += 1
        sib.wait_recv()
        fwd.wait_recv()
        delta = sum_yz(net, tdot(w[...], o[...].reshape(-1, o.shape[2])), sl["ypart1"], sl["ygot1"])
        h_own = (h_own.astype(F32) + delta).astype(BF)
        stats, near, _ = norm_send(net, h_own, sl["hx_m"], sl["ssq_m"])
        window(wn)
        wn += 1
        w = weight("win", l)
        inv = norm_scale(stats, sl["ssq_m"], model_dim)
        near.wait_recv()
        xn = normed(sl["hx_m"].at[0], inv, columns(gx, layers + l))
        r = w.shape[1] // 4
        y = tdot(w[...], xn).astype(BF)
        for d in range(4):
            sl["upart"][slot_of(d)] = y[d * r:(d + 1) * r]
        first = rs_first(net, sl["upart"], sl["ugot"])
        second = rs_second(net, first, sl["upart"], sl["ugot"], sl["uout"], sl["uback"])
        up = rs_last(net, second, sl["upart"], sl["ugot"], sl["uback"]).astype(BF)
        u = sl["u"]
        u[net.i] = jax.nn.gelu(up.astype(F32)).astype(BF)
        sib, across = gather_x(net, u)
        w = weight("wout", l)
        fwd = gather_forward(net, u, across)
        window(wn)
        wn += 1
        sib.wait_recv()
        fwd.wait_recv()
        delta = sum_yz(net, tdot(w[...], u[...].reshape(-1, u.shape[2])), sl["ypart2"], sl["ygot2"])
        h_own = (h_own.astype(F32) + delta).astype(BF)
        end = l == layers - 1
        stats, near, fars = norm_send(net, h_own, s[f"hx_a{l + 1}"], s[f"ssq_a{l + 1}"], far=end)
        if not end:
            window(wn)
            wn += 1
    h_out[...] = h_own.astype(F32).T.astype(BF)
    unembed(net, s, model_dim, 2 * layers, stats, near, fars, g_fars, early, wu_load, s[f"hx_a{layers}"], s[f"ssq_a{layers}"], logit_out)
    net.finish()


def wait_qkv(loads, s, l):
    for c in loads.pop(("qkv", l)):
        c.wait()
    return s[f"wqkv{l}"]


def unembed(net, s, model_dim, gain_row, stats, near, fars, g_fars, early, wu_load, hx, ssq, logit_out):
    v_loc = logit_out.shape[0]
    moved = sum(WINDOWS)
    left = v_loc - moved
    wu, wm, stage = s["wu"], s["wm"], s["stage"]
    inv = norm_scale(stats, ssq, model_dim)
    near.wait_recv()
    xn = normed(hx.at[0], inv, columns(s["gx"], gain_row))
    wu_load.wait()
    far_chip = 1 - net.chip
    send_a, got_a, send_b, got_b = s["send_a"], s["got_a"], s["send_b"], s["got_b"]

    def rows(chip, core, a, n):
        return wu[pl.ds(pl.multiple_of((2 * chip + core) * v_loc + a, 16), n), :]

    def product(chip, core, a, n):
        return jnp.dot(rows(chip, core, moved + a, n), xn, preferred_element_type=F32)

    spans = [(a, min(512, left - a)) for a in range(0, left, 512)]
    first, second = [], []

    def stage1(a, n):
        for chip in range(2):
            send_a[chip, pl.ds(a, n)] = product(chip, 1 - net.core, a, n).astype(BF)
        first.append(net.put(send_a.at[:, pl.ds(a, n)], got_a.at[:, pl.ds(a, n)], net.sib))

    def stage2(r, a, n):
        y = product(far_chip, net.core, a, n)
        first[r].wait_recv()
        send_b[pl.ds(a, n)] = (y + got_a[far_chip, pl.ds(a, n)].astype(F32)).astype(BF)
        second.append(net.put(send_b.at[pl.ds(a, n)], got_b.at[pl.ds(a, n)], net.across))

    stage1(*spans[0])
    for r in range(len(spans)):
        if r + 1 < len(spans):
            stage1(*spans[r + 1])
        stage2(r, *spans[r])

    stores = []

    def store(a, n):
        stores.append(net.fetch(stage.at[pl.ds(a, n)], logit_out.at[pl.ds(a, n)]))

    for c in fars + g_fars + early:
        c.wait_recv()
    xf = normed(hx.at[1], inv, columns(s["gfar"], gain_row))
    x2 = jnp.concatenate([xn, xf], axis=0)
    mspans = [(a, min(512, moved - a)) for a in range(0, moved, 512)]
    send_m, got_m = s["send_m"], s["got_m"]
    third = []

    def both(core, a, n):
        w2 = jnp.concatenate([rows(net.chip, core, a, n), wm[core, pl.ds(a, n), :]], axis=1)
        return jnp.dot(w2, x2, preferred_element_type=F32)

    for a, n in mspans:
        send_m[pl.ds(a, n)] = both(1 - net.core, a, n).astype(BF)
        third.append(net.put(send_m.at[pl.ds(a, n)], got_m.at[pl.ds(a, n)], net.sib))
    for r, (a, n) in enumerate(mspans):
        y = both(net.core, a, n)
        third[r].wait_recv()
        stage[pl.ds(a, n)] = y + got_m[pl.ds(a, n)].astype(F32)
        store(a, n)
    for r, (a, n) in enumerate(spans):
        y = product(net.chip, net.core, a, n) + got_a[net.chip, pl.ds(a, n)].astype(F32)
        second[r].wait_recv()
        stage[pl.ds(moved + a, n)] = y + got_b[pl.ds(a, n)].astype(F32)
        store(moved + a, n)
    for c in stores:
        c.wait()


def scratch(layers, blk, batch, k_o, f_loc, n_qkv, v_loc, width, heads, dh, cache_len):
    r = f_loc // 4
    moved = sum(WINDOWS)
    left = v_loc - moved
    t = {}
    for l in range(layers + 1):
        t[f"hx_a{l}"] = ((2 if l == layers else 1, 2, blk, batch), BF)
        t[f"ssq_a{l}"] = ((8, 1, batch), F32)
    for l in range(layers):
        t.update({
            f"wqkv{l}": ((3, 2 * blk, n_qkv), BF), f"wo{l}": ((k_o, 2 * blk), BF),
            f"win{l}": ((2 * blk, f_loc), BF), f"wout{l}": ((f_loc, 2 * blk), BF),
            f"qkv_part{l}": ((3, 4, width, batch), BF), f"qkv_got{l}": ((3, 2, width, batch), BF),
            f"qkv_out{l}": ((3, width, batch), BF), f"qkv_back{l}": ((3, width, batch), BF),
            f"o{l}": ((4, width, batch), BF),
            f"ypart1{l}": ((2, blk, batch), BF), f"ygot1{l}": ((blk, batch), BF),
            f"hx_m{l}": ((1, 2, blk, batch), BF), f"ssq_m{l}": ((8, 1, batch), F32),
            f"upart{l}": ((4, r, batch), BF), f"ugot{l}": ((2, r, batch), BF),
            f"uout{l}": ((r, batch), BF), f"uback{l}": ((r, batch), BF), f"u{l}": ((4, r, batch), BF),
            f"ypart2{l}": ((2, blk, batch), BF), f"ygot2{l}": ((blk, batch), BF),
        })
    t.update({
        "gx": ((2, 8, blk), F32), "gfar": ((2, 8, blk), F32),
        "q": ((batch, width), F32), "k": ((batch, width), F32), "v": ((batch, width), F32), "att": ((batch, width), F32),
        "kbuf": ((SLOTS, SEQ_STEP, heads, dh, cache_len), BF), "vbuf": ((SLOTS, SEQ_STEP, heads, dh, cache_len), BF),
        "pbuf": ((SEQ_STEP // 8, 16, cache_len), BF), "pnew": ((SEQ_STEP // 8, 16, width), F32),
        "wu": ((4 * v_loc, 2 * blk), BF), "wm": ((2, moved, 2 * blk), BF),
        "send_a": ((2, left, batch), BF), "got_a": ((2, left, batch), BF),
        "send_b": ((left, batch), BF), "got_b": ((left, batch), BF),
        "send_m": ((moved, batch), BF), "got_m": ((moved, batch), BF),
        "stage": ((v_loc, batch), F32),
    })
    return t


def sds(shape, dtype):
    return jax.ShapeDtypeStruct(shape, dtype)


def solution(mesh):
    def decode_step(h_loc, seq_lens, k_cache, v_cache, g_attn, w_q, w_k, w_v, w_o, g_mlp, w_in, w_out, g_final, w_unemb):
        batch, blk = h_loc.shape
        layers = w_q.shape[0]
        heads, dh, cache_len = k_cache.shape[2], k_cache.shape[4], k_cache.shape[3]
        v_loc = w_unemb.shape[1] // 4
        width = heads * dh
        kc = jnp.swapaxes(k_cache, 3, 4)
        vc = jnp.swapaxes(v_cache, 3, 4)
        gains = jnp.concatenate([g_attn, g_mlp, g_final[None]], axis=0).astype(F32)
        gains = jnp.pad(gains, ((0, 8 - gains.shape[0]), (0, 0)))
        names = scratch(layers, blk, batch, w_o.shape[1], w_in.shape[2], w_q.shape[2], v_loc, width, heads, dh, cache_len)
        h_out, logits_t, kt, vt = pl.pallas_call(
            functools.partial(kernel, tuple(names), 8 * blk),
            name="decode",
            out_shape=[sds((batch, blk), BF), sds((v_loc, batch), F32)] + [sds((layers, width, batch), BF)] * 2,
            in_specs=[VM, pl.BlockSpec(memory_space=pltpu.SMEM), ANY, ANY, VM] + [ANY] * 7,
            out_specs=[VM, ANY, VM, VM],
            scratch_shapes=[pltpu.VMEM(shape, dtype) for shape, dtype in names.values()] + [
                pltpu.SemaphoreType.DMA((SLOTS, 2)),
                pltpu.SemaphoreType.DMA((COPIES,)), pltpu.SemaphoreType.DMA((COPIES,)), pltpu.SemaphoreType.DMA((40,))],
            compiler_params=pltpu.CompilerParams(collective_id=0, has_side_effects=True, vmem_limit_bytes=67043328),
        )(h_loc, seq_lens, kc, vc, gains, w_q, w_k, w_v, w_o, w_in, w_out, w_unemb.T)

        def entries(t):
            return jnp.transpose(t.reshape(layers, heads, dh, batch), (0, 3, 1, 2))

        return h_out, logits_t.T, entries(kt), entries(vt)

    emb_spec = P('dp', ('x', 'yz'))
    gain_spec = P(None, ('x', 'yz'))
    cache_spec = P(None, 'dp', ('yz', 'x'), None, None)
    in_rows = P(None, 'x', 'yz')
    out_rows = P(None, 'yz', 'x')
    new_spec = P(None, 'dp', ('yz', 'x'), None)
    in_specs = (emb_spec, P('dp'), cache_spec, cache_spec, gain_spec, in_rows, in_rows, in_rows, out_rows, gain_spec, in_rows, out_rows, P(('x', 'yz')), P('x', 'yz'))
    out_specs = (emb_spec, P('dp', ('yz', 'x')), new_spec, new_spec)
    return jax.shard_map(decode_step, mesh=mesh, in_specs=in_specs, out_specs=out_specs, check_vma=False)
```

time: 467 us -> 156 us (0.33)
  blocking collectives: 178 us -> 0 us
  waiting for transfers between devices: 165 us -> 0 us
  Pallas kernels: 0 us -> 146 us
  matrix products: 75 us -> 0 us
  other arithmetic: 17.6 us -> 1.29 us
  between operations: 14.3 us -> 0.64 us
  local copies, waits for them, and re-layouts: 15 us -> 7.24 us
    pallas_call x0 -> x1, Pallas kernels: none -> 146 us  [decode_step(): pl.pallas_call(functools.partial(kernel, tuple(names), 8 * blk), name='de...]
    psum x5 -> x0, blocking collectives: 114 us -> none  [norm_shard(): lax.psum(jnp.sum(h_f32 * h_f32, axis=-1, keepdims=True), group_axes)]
    reduce_scatter x3 -> x0, waiting for transfers between devices: 101 us -> none  [the longest x1 63.6 us: decode_step(): lax.psum_scatter(matmul_bf16(row_block, w_unemb), 'x', scatter_dimension=...]
    dot_general x17 -> x0, matrix products: 75 us -> none  [the longest x2 28.2 us: attend(): jnp.einsum('bhs,bhsd->bhd', p_cache, v_cache, preferred_element_type=jnp....]
    unnamed x23 -> x0, waiting for transfers between devices: 63.9 us -> none
    all_gather x9 -> x0, blocking collectives: 63.4 us -> none  [the longest x5 26.2 us: decode_step(): row_block = lax.all_gather(normed, 'yz', axis=1, tiled=True)]
    convert_element_type x15 -> x0, other arithmetic: 9.81 us -> none  [the longest x1 3.88 us: decode_step(): lax.psum_scatter(matmul_bf16(row_block, w_unemb), 'x', scatter_dimension=...]
    unnamed x42 -> x8, local copies, waits for them, and re-layouts: 12.8 us -> 7.24 us
  transfers between devices with their start and end apart: 13 -> 0, of which waited for: 13 -> 0; matrix products, arithmetic and copies ran while one was open for 15% -> 0% of each run, Pallas kernels for 0% -> 0%
where the time goes in v2:
time: 156 us
  Pallas kernels  146 us (94%)
  local copies, waits for them, and re-layouts  7.24 us (5%)
    pallas_call x1, Pallas kernels, decode_step(): pl.pallas_call(functools.partial(kernel, tuple(names), 8 * blk), name='de...  146 us
    unnamed x8, local copies, waits for them, and re-layouts  7.24 us

profile of v2, /device:TPU:0, one launch (start us, length us, event | category | flops | bytes accessed | tf_op | source)
XLA Modules:
  0.0 155.5 jit_solution(10162500845398106765)
XLA Ops:
  0.6 1.3 fusion.5.g_ref
  1.9 146.4 %decode.1 = (bf16[256,128]{1,0:T(8,128)(2,1)}, f32[4016,256]{1,0:T(8,128)}, bf16[2,128,256]{2,1,0:T(8,128)(2,1)}, bf16[2,128,256]{2,1,0:T(8,128)(2,1)}) custom-call(bf16[256,128]{1,0:T(8,128)(2,1)} %h_ref.1, s32[256]{0:T(256)} %lens_ref.1, bf16[2,256,2,64,512]{4,3,2,1,0:T(8,128)(2,1)} %bitcast.kc, bf16[2,256,2,64,512]{4,3,2,1,0:T(8,128)(2,1)} %bitcast.1.vc, ...), custom_call_target="tpu_custom_call" | custom-call | tf_op jit(solution)/shard_map/decode/pallas_call | solution.py:497
  148.3 1.5 copy.22
  149.8 0.0 copy-start.1
  149.8 0.0 copy-start
  149.8 4.5 %copy.23 = f32[256,4016]{0,1:T(8,128)} copy(f32[256,4016]{0,1:T(8,128)} %bitcast.12) | data formatting | bytes 8224768
  154.2 0.0 copy-done.1
  154.2 0.7 copy.24
  154.9 0.0 copy-done
  154.9 0.7 copy.25
Async XLA Ops:
  149.8 4.5 %copy-start.1 = (bf16[2,128,256]{2,1,0:T(8,128)(2,1)S(1)}, bf16[2,128,256]{2,1,0:T(8,128)(2,1)}, u32[]{:S(2)}) copy-start(bf16[2,128,256]{2,1,0:T(8,128)(2,1)} %get-tuple-element.10) | copy-start | bytes 393220
  149.8 5.1 %copy-start = (bf16[2,128,256]{2,1,0:T(8,128)(2,1)S(1)}, bf16[2,128,256]{2,1,0:T(8,128)(2,1)}, u32[]{:S(2)}) copy-start(bf16[2,128,256]{2,1,0:T(8,128)(2,1)} %get-tuple-element.11) | copy-start | bytes 393220

commit v3 on v2

--- a/solution.py
+++ b/solution.py
@@ -15,8 +15,9 @@
 VM = pl.BlockSpec(memory_space=pltpu.VMEM)
 SEQ_STEP = 16
 SLOTS = 5
-WINDOWS = (768, 176, 208, 224, 240, 768, 176, 208, 224)
-COPIES = 150
+WINDOWS = (176, 768, 176, 240, 208, 288, 768, 176, 240, 208, 128)
+COPIES = 170
+OUT_ROWS = 512
 
 
 def tdot(w, act):
@@ -225,13 +226,13 @@
     return net.put(far, far, net.sib)
 
 
-def sum_yz(net, y, part, got):
-    r = y.shape[0] // 2
-    part[0] = y[:r].astype(BF)
-    part[1] = y[r:].astype(BF)
-    c = net.put(part.at[1 - net.j], got, net.yother)
+def sum_yz(net, w, act, part, got):
+    r = got.shape[0]
+    part[...] = tdot(w[:, pl.ds(pl.multiple_of((1 - net.j) * r, r), r)], act).astype(BF)
+    c = net.put(part, got, net.yother)
+    mine = tdot(w[:, pl.ds(pl.multiple_of(net.j * r, r), r)], act)
     c.wait_recv()
-    return part[net.j].astype(F32) + got[...].astype(F32)
+    return mine + got[...].astype(F32)
 
 
 def norm_send(net, h_own, hx, ssq, far=False):
@@ -268,7 +269,7 @@
     return jnp.concatenate([gx[0].T[:, n:n + 1], gx[1].T[:, n:n + 1]], axis=0)
 
 
-def kernel(names, model_dim, h_ref, lens_ref, kc, vc, g_ref, wq, wk, wv, wo, win, wout, wu, h_out, logit_out, kt_out, vt_out, *rest):
+def kernel(names, model_dim, h_ref, lens_ref, kc, vc, ga, gm, gf, wq, wk, wv, wo, win, wout, wu, h_out, p_own, p_other, kt_out, vt_out, *rest):
     s = dict(zip(names, rest))
     kv_sems, send, recv, local = rest[len(names):]
     layers = wq.shape[0]
@@ -289,7 +290,7 @@
             c.wait()
         return s[f"{name}{l}"]
 
-    v_loc = logit_out.shape[0]
+    v_loc = p_own.shape[0]
     early = []
     far_chip = 1 - net.chip
 
@@ -301,19 +302,25 @@
 
     gx, gfar = s["gx"], s["gfar"]
     h_own = h_ref[...].astype(F32).T.astype(BF)
-    gx[net.j] = g_ref[...]
+    for n, g in enumerate((ga, gm, gf)):
+        gx[net.j, pl.ds(n * layers, g.shape[0])] = g[...].astype(F32)
+    rest_rows = gx.shape[1] - 2 * layers - 1
+    gx[net.j, pl.ds(2 * layers + 1, rest_rows)] = jnp.zeros((rest_rows, gx.shape[2]), F32)
     net.met()
     g_near = net.put(gx.at[net.j], gx.at[net.j], net.yother)
     stats, near, _ = norm_send(net, h_own, s["hx_a0"], s["ssq_a0"])
     g_fars = [net.put(gx.at[net.j], gfar.at[net.j], to) for to in (net.across, net.peer(2, 1))]
+    window(0)
     g_near.wait_recv()
-    wn = 0
+    wn = 1
+    stores = []
     for l in range(layers):
         inv = norm_scale(stats, s[f"ssq_a{l}"], model_dim)
         near.wait_recv()
         xn = normed(s[f"hx_a{l}"].at[0], inv, columns(gx, l))
         sl = {k[:-1]: s[k] for k in s if k.endswith(str(l))}
-        qkv_stage(net, xn, wait_qkv(loads, s, l), sl, s["q"], s["k"], s["v"], kt_out.at[l], vt_out.at[l])
+        qkv_stage(net, xn, wait_qkv(loads, s, l), sl, s["q"], s["k"], s["v"], s["kt"].at[l], s["vt"].at[l])
+        stores += [net.fetch(s["kt"].at[l], kt_out.at[l]), net.fetch(s["vt"].at[l], vt_out.at[l])]
         window(wn)
         wn += 1
         att.layer(l)
@@ -328,7 +335,7 @@
         wn += 1
         sib.wait_recv()
         fwd.wait_recv()
-        delta = sum_yz(net, tdot(w[...], o[...].reshape(-1, o.shape[2])), sl["ypart1"], sl["ygot1"])
+        delta = sum_yz(net, w, o[...].reshape(-1, o.shape[2]), sl["ypart1"], sl["ygot1"])
         h_own = (h_own.astype(F32) + delta).astype(BF)
         stats, near, _ = norm_send(net, h_own, sl["hx_m"], sl["ssq_m"])
         window(wn)
@@ -341,27 +348,34 @@
         y = tdot(w[...], xn).astype(BF)
         for d in range(4):
             sl["upart"][slot_of(d)] = y[d * r:(d + 1) * r]
-        first = rs_first(net, sl["upart"], sl["ugot"])
-        second = rs_second(net, first, sl["upart"], sl["ugot"], sl["uout"], sl["uback"])
-        up = rs_last(net, second, sl["upart"], sl["ugot"], sl["uback"]).astype(BF)
         u = sl["u"]
-        u[net.i] = jax.nn.gelu(up.astype(F32)).astype(BF)
-        sib, across = gather_x(net, u)
-        w = weight("wout", l)
-        fwd = gather_forward(net, u, across)
+        half = [pl.ds(n * (r // 2), r // 2) for n in range(2)]
+        pieces = [[sl[k].at[:, h] for k in ("upart", "ugot")] + [sl[k].at[h] for k in ("uout", "uback")] for h in half]
+        first = [rs_first(net, part, got) for part, got, out, back in pieces]
+        second = [rs_second(net, first[n], *p) for n, p in enumerate(pieces)]
+        sent = []
+        for n, (part, got, out, back) in enumerate(pieces):
+            up = rs_last(net, second[n], part, got, back).astype(BF)
+            u[net.i, half[n]] = jax.nn.gelu(up.astype(F32)).astype(BF)
+            sent.append(gather_x(net, u.at[:, half[n]]))
         window(wn)
         wn += 1
-        sib.wait_recv()
-        fwd.wait_recv()
-        delta = sum_yz(net, tdot(w[...], u[...].reshape(-1, u.shape[2])), sl["ypart2"], sl["ygot2"])
+        w = weight("wout", l)
+        fwd = [gather_forward(net, u.at[:, half[n]], sent[n][1]) for n in range(2)]
+        for n in range(2):
+            sent[n][0].wait_recv()
+            fwd[n].wait_recv()
+        delta = sum_yz(net, w, u[...].reshape(-1, u.shape[2]), sl["ypart2"], sl["ygot2"])
         h_own = (h_own.astype(F32) + delta).astype(BF)
         end = l == layers - 1
         stats, near, fars = norm_send(net, h_own, s[f"hx_a{l + 1}"], s[f"ssq_a{l + 1}"], far=end)
-        if not end:
-            window(wn)
-            wn += 1
-    h_out[...] = h_own.astype(F32).T.astype(BF)
-    unembed(net, s, model_dim, 2 * layers, stats, near, fars, g_fars, early, wu_load, s[f"hx_a{layers}"], s[f"ssq_a{layers}"], logit_out)
+        window(wn)
+        wn += 1
+    s["h"][...] = h_own.astype(F32).T.astype(BF)
+    stores.append(net.fetch(s["h"], h_out))
+    unembed(net, s, model_dim, 2 * layers, stats, near, fars, g_fars, early, wu_load, s[f"hx_a{layers}"], s[f"ssq_a{layers}"], p_own, p_other, stores)
+    for c in stores:
+        c.wait()
     net.finish()
 
 
@@ -371,17 +385,17 @@
     return s[f"wqkv{l}"]
 
 
-def unembed(net, s, model_dim, gain_row, stats, near, fars, g_fars, early, wu_load, hx, ssq, logit_out):
-    v_loc = logit_out.shape[0]
+def unembed(net, s, model_dim, gain_row, stats, near, fars, g_fars, early, wu_load, hx, ssq, p_own, p_other, stores):
+    v_loc = p_own.shape[0]
     moved = sum(WINDOWS)
     left = v_loc - moved
-    wu, wm, stage = s["wu"], s["wm"], s["stage"]
+    wu, wm, own = s["wu"], s["wm"], s["own"]
     inv = norm_scale(stats, ssq, model_dim)
     near.wait_recv()
     xn = normed(hx.at[0], inv, columns(s["gx"], gain_row))
     wu_load.wait()
     far_chip = 1 - net.chip
-    send_a, got_a, send_b, got_b = s["send_a"], s["got_a"], s["send_b"], s["got_b"]
+    send_a, got_a, send_b = s["send_a"], s["got_a"], s["send_b"]
 
     def rows(chip, core, a, n):
         return wu[pl.ds(pl.multiple_of((2 * chip + core) * v_loc + a, 16), n), :]
@@ -390,7 +404,7 @@
         return jnp.dot(rows(chip, core, moved + a, n), xn, preferred_element_type=F32)
 
     spans = [(a, min(512, left - a)) for a in range(0, left, 512)]
-    first, second = [], []
+    first, arrivals = [], []
 
     def stage1(a, n):
         for chip in range(2):
@@ -401,7 +415,7 @@
         y = product(far_chip, net.core, a, n)
         first[r].wait_recv()
         send_b[pl.ds(a, n)] = (y + got_a[far_chip, pl.ds(a, n)].astype(F32)).astype(BF)
-        second.append(net.put(send_b.at[pl.ds(a, n)], got_b.at[pl.ds(a, n)], net.across))
+        arrivals.append(net.put(send_b.at[pl.ds(a, n)], p_other.at[pl.ds(moved + a, n)], net.across))
 
     stage1(*spans[0])
     for r in range(len(spans)):
@@ -409,18 +423,15 @@
             stage1(*spans[r + 1])
         stage2(r, *spans[r])
 
-    stores = []
-
     def store(a, n):
-        stores.append(net.fetch(stage.at[pl.ds(a, n)], logit_out.at[pl.ds(a, n)]))
+        stores.append(net.fetch(own.at[pl.ds(a, n)], p_own.at[pl.ds(a, n)]))
 
     for c in fars + g_fars + early:
         c.wait_recv()
     xf = normed(hx.at[1], inv, columns(s["gfar"], gain_row))
     x2 = jnp.concatenate([xn, xf], axis=0)
     mspans = [(a, min(512, moved - a)) for a in range(0, moved, 512)]
-    send_m, got_m = s["send_m"], s["got_m"]
-    third = []
+    send_m = s["send_m"]
 
     def both(core, a, n):
         w2 = jnp.concatenate([rows(net.chip, core, a, n), wm[core, pl.ds(a, n), :]], axis=1)
@@ -428,18 +439,38 @@
 
     for a, n in mspans:
         send_m[pl.ds(a, n)] = both(1 - net.core, a, n).astype(BF)
-        third.append(net.put(send_m.at[pl.ds(a, n)], got_m.at[pl.ds(a, n)], net.sib))
-    for r, (a, n) in enumerate(mspans):
-        y = both(net.core, a, n)
-        third[r].wait_recv()
-        stage[pl.ds(a, n)] = y + got_m[pl.ds(a, n)].astype(F32)
+        arrivals.append(net.put(send_m.at[pl.ds(a, n)], p_other.at[pl.ds(a, n)], net.sib))
+    for a, n in mspans:
+        own[pl.ds(a, n)] = both(net.core, a, n).astype(BF)
         store(a, n)
-    for r, (a, n) in enumerate(spans):
+    for a, n in spans:
         y = product(net.chip, net.core, a, n) + got_a[net.chip, pl.ds(a, n)].astype(F32)
-        second[r].wait_recv()
-        stage[pl.ds(moved + a, n)] = y + got_b[pl.ds(a, n)].astype(F32)
+        own[pl.ds(moved + a, n)] = y.astype(BF)
         store(moved + a, n)
-    for c in stores:
+    for c in arrivals:
+        c.wait_recv()
+
+
+def output_kernel(p_own, p_other, h, kt, vt, logits, h_out, kt_out, vt_out, own, other, total, hb, kb, vb, in_sems, out_sems):
+    small = [(h, hb, h_out), (kt, kb, kt_out), (vt, vb, vt_out)]
+    spans = [pl.ds(a, min(OUT_ROWS, total.shape[0] - a)) for a in range(0, total.shape[0], OUT_ROWS)]
+    ins = [[pltpu.make_async_copy(p.at[d], buf.at[d], in_sems.at[2 * n + m]) for m, (p, buf) in enumerate(((p_own, own), (p_other, other)))]
+           for n, d in enumerate(spans)]
+    ins += [[pltpu.make_async_copy(src, buf, in_sems.at[2 * len(spans) + n])] for n, (src, buf, dst) in enumerate(small)]
+    outs = [pltpu.make_async_copy(total.at[d], logits.at[d], out_sems.at[n]) for n, d in enumerate(spans)]
+    outs += [pltpu.make_async_copy(buf, dst, out_sems.at[len(spans) + n]) for n, (src, buf, dst) in enumerate(small)]
+    for group in ins:
+        for c in group:
+            c.start()
+    for n, d in enumerate(spans):
+        for c in ins[n]:
+            c.wait()
+        total[d] = own[d].astype(F32) + other[d].astype(F32)
+        outs[n].start()
+    for n in range(len(small)):
+        ins[len(spans) + n][0].wait()
+        outs[len(spans) + n].start()
+    for c in outs:
         c.wait()
 
 
@@ -458,11 +489,11 @@
             f"qkv_part{l}": ((3, 4, width, batch), BF), f"qkv_got{l}": ((3, 2, width, batch), BF),
             f"qkv_out{l}": ((3, width, batch), BF), f"qkv_back{l}": ((3, width, batch), BF),
             f"o{l}": ((4, width, batch), BF),
-            f"ypart1{l}": ((2, blk, batch), BF), f"ygot1{l}": ((blk, batch), BF),
+            f"ypart1{l}": ((blk, batch), BF), f"ygot1{l}": ((blk, batch), BF),
             f"hx_m{l}": ((1, 2, blk, batch), BF), f"ssq_m{l}": ((8, 1, batch), F32),
             f"upart{l}": ((4, r, batch), BF), f"ugot{l}": ((2, r, batch), BF),
             f"uout{l}": ((r, batch), BF), f"uback{l}": ((r, batch), BF), f"u{l}": ((4, r, batch), BF),
-            f"ypart2{l}": ((2, blk, batch), BF), f"ygot2{l}": ((blk, batch), BF),
+            f"ypart2{l}": ((blk, batch), BF), f"ygot2{l}": ((blk, batch), BF),
         })
     t.update({
         "gx": ((2, 8, blk), F32), "gfar": ((2, 8, blk), F32),
@@ -471,9 +502,8 @@
         "pbuf": ((SEQ_STEP // 8, 16, cache_len), BF), "pnew": ((SEQ_STEP // 8, 16, width), F32),
         "wu": ((4 * v_loc, 2 * blk), BF), "wm": ((2, moved, 2 * blk), BF),
         "send_a": ((2, left, batch), BF), "got_a": ((2, left, batch), BF),
-        "send_b": ((left, batch), BF), "got_b": ((left, batch), BF),
-        "send_m": ((moved, batch), BF), "got_m": ((moved, batch), BF),
-        "stage": ((v_loc, batch), F32),
+        "send_b": ((left, batch), BF), "send_m": ((moved, batch), BF), "own": ((v_loc, batch), BF),
+        "kt": ((layers, width, batch), BF), "vt": ((layers, width, batch), BF), "h": ((batch, blk), BF),
     })
     return t
 
@@ -491,20 +521,31 @@
         width = heads * dh
         kc = jnp.swapaxes(k_cache, 3, 4)
         vc = jnp.swapaxes(v_cache, 3, 4)
-        gains = jnp.concatenate([g_attn, g_mlp, g_final[None]], axis=0).astype(F32)
-        gains = jnp.pad(gains, ((0, 8 - gains.shape[0]), (0, 0)))
         names = scratch(layers, blk, batch, w_o.shape[1], w_in.shape[2], w_q.shape[2], v_loc, width, heads, dh, cache_len)
-        h_out, logits_t, kt, vt = pl.pallas_call(
+        h_out, p_own, p_other, kt, vt = pl.pallas_call(
             functools.partial(kernel, tuple(names), 8 * blk),
             name="decode",
-            out_shape=[sds((batch, blk), BF), sds((v_loc, batch), F32)] + [sds((layers, width, batch), BF)] * 2,
-            in_specs=[VM, pl.BlockSpec(memory_space=pltpu.SMEM), ANY, ANY, VM] + [ANY] * 7,
-            out_specs=[VM, ANY, VM, VM],
+            out_shape=[sds((batch, blk), BF), sds((v_loc, batch), BF), sds((v_loc, batch), BF)] + [sds((layers, width, batch), BF)] * 2,
+            in_specs=[VM, pl.BlockSpec(memory_space=pltpu.SMEM), ANY, ANY, VM, VM, VM] + [ANY] * 7,
+            out_specs=[ANY] * 5,
             scratch_shapes=[pltpu.VMEM(shape, dtype) for shape, dtype in names.values()] + [
                 pltpu.SemaphoreType.DMA((SLOTS, 2)),
                 pltpu.SemaphoreType.DMA((COPIES,)), pltpu.SemaphoreType.DMA((COPIES,)), pltpu.SemaphoreType.DMA((40,))],
             compiler_params=pltpu.CompilerParams(collective_id=0, has_side_effects=True, vmem_limit_bytes=67043328),
-        )(h_loc, seq_lens, kc, vc, gains, w_q, w_k, w_v, w_o, w_in, w_out, w_unemb.T)
+        )(h_loc, seq_lens, kc, vc, g_attn, g_mlp, g_final[None], w_q, w_k, w_v, w_o, w_in, w_out, w_unemb.T)
+
+        parts = -(-v_loc // OUT_ROWS)
+        logits_t, h_out, kt, vt = pl.pallas_call(
+            output_kernel,
+            name="outputs",
+            out_shape=[sds((v_loc, batch), F32), sds(h_out.shape, BF), sds(kt.shape, BF), sds(vt.shape, BF)],
+            in_specs=[ANY] * 5,
+            out_specs=[ANY] * 4,
+            scratch_shapes=[pltpu.VMEM((v_loc, batch), BF), pltpu.VMEM((v_loc, batch), BF), pltpu.VMEM((v_loc, batch), F32),
+                            pltpu.VMEM(h_out.shape, BF), pltpu.VMEM(kt.shape, BF), pltpu.VMEM(vt.shape, BF),
+                            pltpu.SemaphoreType.DMA((2 * parts + 3,)), pltpu.SemaphoreType.DMA((parts + 3,))],
+            compiler_params=pltpu.CompilerParams(vmem_limit_bytes=56 * 2**20),
+        )(p_own, p_other, h_out, kt, vt)
 
         def entries(t):
             return jnp.transpose(t.reshape(layers, heads, dh, batch), (0, 3, 1, 2))

time: 156 us -> 143 us (0.917)
  local copies, waits for them, and re-layouts: 7.24 us -> 0 us
  Pallas kernels: 146 us -> 142 us
    pallas_call x1, Pallas kernels: 146 us -> 139 us  [decode_step(): pl.pallas_call(functools.partial(kernel, tuple(names), 8 * blk), name='de...]
    unnamed x8 -> x0, local copies, waits for them, and re-layouts: 7.24 us -> none
    pallas_call x0 -> x1, Pallas kernels: none -> 3.69 us  [decode_step(): pl.pallas_call(output_kernel, name='outputs', out_shape=[sds((v_loc, batc...]
where the time goes in v3:
time: 143 us
  Pallas kernels  142 us (99%)
    pallas_call x1, Pallas kernels, decode_step(): pl.pallas_call(functools.partial(kernel, tuple(names), 8 * blk), name='de...  139 us
    pallas_call x1, Pallas kernels, decode_step(): pl.pallas_call(output_kernel, name='outputs', out_shape=[sds((v_loc, batc...  3.69 us

profile of v3, /device:TPU:0, one launch (start us, length us, event | category | flops | bytes accessed | tf_op | source)
XLA Modules:
  0.0 143.1 jit_solution(13895126387379254326)
XLA Ops:
  0.6 138.7 %decode.1 = (bf16[256,128]{1,0:T(8,128)(2,1)}, bf16[4016,256]{1,0:T(8,128)(2,1)}, bf16[4016,256]{1,0:T(8,128)(2,1)}, bf16[2,128,256]{2,1,0:T(8,128)(2,1)}, bf16[2,128,256]{2,1,0:T(8,128)(2,1)}) custom-call(bf16[256,128]{1,0:T(8,128)(2,1)} %h_ref.1, s32[256]{0:T(256)} %lens_ref.1, bf16[2,256,2,64,512]{4,3,2,1,0:T(8,128)(2,1)} %bitcast.kc, ...), custom_call_target="tpu_custom_call" | custom-call | tf_op jit(solution)/shard_map/decode/pallas_call | solution.py:525
  139.4 3.7 %outputs.1 = (f32[4016,256]{1,0:T(8,128)}, bf16[256,128]{1,0:T(8,128)(2,1)}, bf16[2,128,256]{2,1,0:T(8,128)(2,1)}, bf16[2,128,256]{2,1,0:T(8,128)(2,1)}) custom-call(bf16[4016,256]{1,0:T(8,128)(2,1)} %get-tuple-element.13.p_own, bf16[4016,256]{1,0:T(8,128)(2,1)} %get-tuple-element.14.p_other, bf16[256,128]{1,0:T(8,128)(2,1)} %get-tuple-element.15.h, ...), custom_call_target="tpu_custom_call" | custom-call | tf_op jit(solution)/shard_map/outputs/pallas_call | solution.py:538

commit v4 on v3

--- a/solution.py
+++ b/solution.py
@@ -15,8 +15,11 @@
 VM = pl.BlockSpec(memory_space=pltpu.VMEM)
 SEQ_STEP = 16
 SLOTS = 5
-WINDOWS = (176, 768, 176, 240, 208, 288, 768, 176, 240, 208, 128)
-COPIES = 170
+HALVES = 2
+PARTS = 4
+MOVED = 3168
+PIECE = 96
+COPIES = 250
 OUT_ROWS = 512
 
 
@@ -97,35 +100,47 @@
             o2 = o2 + self.pnew[g] * jnp.concatenate([v8, v8], axis=0)
             self.o[pl.ds(self.base(step, g), 8), :] = jnp.where(self.first_head, o2[:8], o2[8:])
 
-    def layer(self, layer):
+    def fetched(self, g, n):
+        self.copy(g, n).wait()
+        return lax.rem(g, SLOTS)
+
+    def refill(self, g):
+        nxt = g - 2 + SLOTS
+
+        @pl.when((g >= 2) & (nxt < self.layers * self.steps))
+        def _():
+            self.issue(nxt)
+
+    def piece(self, layer, half, n, count):
         first = layer * self.steps
-        last = self.layers * self.steps
-
-        def fetched(step, n):
-            self.copy(first + step, n).wait()
-            return lax.rem(first + step, SLOTS)
-
-        self.softmax(0, *self.score(0, fetched(jnp.int32(0), 0)))
+        per = self.steps // HALVES
+        lo = half * per
+        begin, end = lo + n * per // count, lo + (n + 1) * per // count
 
         def body(step, carry):
-            nxt = first + step - 2 + SLOTS
-
-            @pl.when((step >= 2) & (nxt < last))
-            def _():
-                self.issue(nxt)
-
-            k_slot = fetched(step, 0)
-            v_slot = fetched(step - 1, 1)
+            self.refill(first + step)
+            k_slot = self.fetched(first + step, 0)
+            v_slot = self.fetched(first + step - 1, 1)
             q2s, scores = self.score(step, k_slot)
             self.mix(step - 1, v_slot)
             self.softmax(step, q2s, scores)
             return carry
 
-        lax.fori_loop(1, self.steps, body, 0)
-        self.mix(self.steps - 1, fetched(jnp.int32(self.steps - 1), 1))
-        for g in (first + self.steps - 2 + SLOTS, first + self.steps - 1 + SLOTS):
-            if g < last:
-                self.issue(jnp.int32(g))
+        if n == 0:
+            self.refill(jnp.int32(first + begin))
+            self.softmax(begin, *self.score(begin, self.fetched(jnp.int32(first + begin), 0)))
+            begin += 1
+        lax.fori_loop(begin, end, body, 0)
+        if n == count - 1:
+            self.mix(end - 1, self.fetched(jnp.int32(first + end - 1), 1))
+
+
+class Message:
+    def __init__(self, copy, arrives):
+        self.copy, self.arrives = copy, arrives
+
+    def wait_recv(self):
+        self.copy.wait_recv()
 
 
 class Net:
@@ -141,6 +156,8 @@
         self.n = 0
         self.m = 0
         self.sent = []
+        self.now = 0.0
+        self.free = {"x": 0.0, "y": 0.0, "d": 0.0}
 
     def greet(self):
         self.barrier = pltpu.get_barrier_semaphore()
@@ -162,7 +179,18 @@
         self.n += 1
         c.start()
         self.sent.append(c)
-        return c
+        size = src.dtype.itemsize
+        for d in src.shape:
+            size *= d
+        if to is self.sib:
+            link, rate, latency = "d", 600e3, 1.0
+        elif to is self.yother:
+            link, rate, latency = "y", 46e3, 1.8
+        else:
+            link, rate, latency = "x", 46e3, 1.8
+        begin = max(self.now, self.free[link])
+        self.free[link] = begin + size / rate
+        return Message(c, self.free[link] + latency)
 
     def fetch(self, src, dst):
         c = pltpu.make_async_copy(src, dst, self.local.at[self.m])
@@ -175,6 +203,27 @@
             c.wait_send()
 
 
+def interleave(net, chains, fill):
+    state = []
+    for c in chains:
+        state.append([net.now, 0.0, [], c, None])
+    turn = 0
+    while state:
+        best = min((e for e in state if e[4] in (None, turn)), key=lambda e: (max(net.now, e[0]), e[0]))
+        turn += best[4] is not None
+        begin = max(net.now, best[0])
+        fill(begin + best[1])
+        for m in best[2]:
+            m.wait_recv()
+        net.now = begin + best[1]
+        try:
+            best[2], best[1], *tail = next(best[3])
+            best[4] = tail[0] if tail else None
+            best[0] = max([net.now] + [m.arrives for m in best[2]])
+        except StopIteration:
+            state.remove(best)
+
+
 def slot_of(d):
     return 2 * (d % 2) + d // 2
 
@@ -183,34 +232,14 @@
     return net.put(part.at[pl.ds(2 * (1 - net.core), 2)], got, net.sib)
 
 
-def rs_second(net, wait, part, got, out, back):
-    wait.wait_recv()
+def rs_second(net, part, got, out, back):
     far = 1 - net.chip
     out[...] = (part[2 * net.core + far].astype(F32) + got[far].astype(F32)).astype(BF)
     return net.put(out, back, net.across)
 
 
-def rs_last(net, wait, part, got, back):
-    mine = part[2 * net.core + net.chip].astype(F32) + got[net.chip].astype(F32)
-    wait.wait_recv()
-    return mine + back[...].astype(F32)
-
-
-def qkv_stage(net, xn, w, s, q_out, k_out, v_out, kt_out, vt_out):
-    part, got, out, back = s["qkv_part"], s["qkv_got"], s["qkv_out"], s["qkv_back"]
-    first = []
-    for n in range(3):
-        y = tdot(w[n], xn).astype(BF)
-        r = y.shape[0] // 4
-        for d in range(4):
-            part[n, slot_of(d)] = y[d * r:(d + 1) * r]
-        first.append(rs_first(net, part.at[n], got.at[n]))
-    second = [rs_second(net, first[n], part.at[n], got.at[n], out.at[n], back.at[n]) for n in range(3)]
-    for n in range(3):
-        y = rs_last(net, second[n], part.at[n], got.at[n], back.at[n]).astype(BF)
-        if n:
-            (kt_out, vt_out)[n - 1][...] = y
-        (q_out, k_out, v_out)[n][...] = y.astype(F32).T
+def rs_last(net, part, got, back):
+    return part[2 * net.core + net.chip].astype(F32) + got[net.chip].astype(F32) + back[...].astype(F32)
 
 
 def gather_x(net, buf):
@@ -220,19 +249,19 @@
     return sib, across
 
 
-def gather_forward(net, buf, across):
-    across.wait_recv()
+def gather_forward(net, buf):
     far = buf.at[lax.rem(net.i + 2, 4)]
     return net.put(far, far, net.sib)
 
 
-def sum_yz(net, w, act, part, got):
+def send_half(net, w, act, part, got):
     r = got.shape[0]
     part[...] = tdot(w[:, pl.ds(pl.multiple_of((1 - net.j) * r, r), r)], act).astype(BF)
-    c = net.put(part, got, net.yother)
-    mine = tdot(w[:, pl.ds(pl.multiple_of(net.j * r, r), r)], act)
-    c.wait_recv()
-    return mine + got[...].astype(F32)
+    return net.put(part, got, net.yother)
+
+
+def own_half(net, w, act, r):
+    return tdot(w[:, pl.ds(pl.multiple_of(net.j * r, r), r)], act)
 
 
 def norm_send(net, h_own, hx, ssq, far=False):
@@ -251,9 +280,7 @@
     return stats, near, fars
 
 
-def norm_scale(stats, ssq, model_dim):
-    for c in stats:
-        c.wait_recv()
+def norm_scale(ssq, model_dim):
     total = ssq[0]
     for n in range(1, 8):
         total = total + ssq[n]
@@ -276,123 +303,163 @@
     net = Net(send, recv, local)
     net.greet()
     mats = (("wo", wo), ("win", win), ("wout", wout))
-    loads = {("qkv", 0): [net.fetch(w.at[0], s["wqkv0"].at[n]) for n, w in enumerate((wq, wk, wv))]}
+    loads = {("wqkv", 0): [net.fetch(w.at[0], s["wqkv0"].at[n]) for n, w in enumerate((wq, wk, wv))]}
     att = Attention(lens_ref, kc, vc, s["q"], s["k"], s["v"], s["att"], s["kbuf"], s["vbuf"], s["pbuf"], s["pnew"], kv_sems)
     for l in range(layers):
         if l:
-            loads["qkv", l] = [net.fetch(w.at[l], s[f"wqkv{l}"].at[n]) for n, w in enumerate((wq, wk, wv))]
+            loads["wqkv", l] = [net.fetch(w.at[l], s[f"wqkv{l}"].at[n]) for n, w in enumerate((wq, wk, wv))]
         for name, w in mats:
             loads[name, l] = [net.fetch(w.at[l], s[f"{name}{l}"])]
     att.start()
 
-    def weight(name, l):
-        for c in loads.pop((name, l)):
-            c.wait()
-        return s[f"{name}{l}"]
-
     v_loc = p_own.shape[0]
     early = []
     far_chip = 1 - net.chip
 
-    def window(n):
-        a = sum(WINDOWS[:n])
-        for core in range(2):
-            src = wu.at[pl.ds(pl.multiple_of((2 * far_chip + core) * v_loc + a, 16), WINDOWS[n])]
-            early.append(net.put(src, s["wm"].at[core, pl.ds(a, WINDOWS[n])], net.across))
+    def cross():
+        core, a = len(early) % 2, len(early) // 2 * PIECE
+        src = wu.at[pl.ds(pl.multiple_of((2 * far_chip + core) * v_loc + a, 16), PIECE)]
+        early.append(net.put(src, s["wm"].at[core, pl.ds(a, PIECE)], net.across))
+
+    cost = PIECE * 512 / 46e3
+
+    def fill(until):
+        while len(early) < 2 * MOVED // PIECE and net.free["x"] + cost <= until:
+            net.free["x"] = max(net.free["x"], net.now)
+            if net.free["x"] + cost > until:
+                break
+            cross()
 
     gx, gfar = s["gx"], s["gfar"]
-    h_own = h_ref[...].astype(F32).T.astype(BF)
     for n, g in enumerate((ga, gm, gf)):
         gx[net.j, pl.ds(n * layers, g.shape[0])] = g[...].astype(F32)
     rest_rows = gx.shape[1] - 2 * layers - 1
     gx[net.j, pl.ds(2 * layers + 1, rest_rows)] = jnp.zeros((rest_rows, gx.shape[2]), F32)
+    h_in = h_ref[...].astype(F32).T.astype(BF)
     net.met()
     g_near = net.put(gx.at[net.j], gx.at[net.j], net.yother)
-    stats, near, _ = norm_send(net, h_own, s["hx_a0"], s["ssq_a0"])
-    g_fars = [net.put(gx.at[net.j], gfar.at[net.j], to) for to in (net.across, net.peer(2, 1))]
-    window(0)
-    g_near.wait_recv()
-    wn = 1
+    g_fars = []
     stores = []
-    for l in range(layers):
-        inv = norm_scale(stats, s[f"ssq_a{l}"], model_dim)
-        near.wait_recv()
-        xn = normed(s[f"hx_a{l}"].at[0], inv, columns(gx, l))
-        sl = {k[:-1]: s[k] for k in s if k.endswith(str(l))}
-        qkv_stage(net, xn, wait_qkv(loads, s, l), sl, s["q"], s["k"], s["v"], s["kt"].at[l], s["vt"].at[l])
-        stores += [net.fetch(s["kt"].at[l], kt_out.at[l]), net.fetch(s["vt"].at[l], vt_out.at[l])]
-        window(wn)
-        wn += 1
-        att.layer(l)
-        if l == layers - 1:
-            wu_load = net.fetch(wu, s["wu"])
-        o = sl["o"]
-        o[net.i] = s["att"][...].T.astype(BF)
-        sib, across = gather_x(net, o)
-        w = weight("wo", l)
-        fwd = gather_forward(net, o, across)
-        window(wn)
-        wn += 1
-        sib.wait_recv()
-        fwd.wait_recv()
-        delta = sum_yz(net, w, o[...].reshape(-1, o.shape[2]), sl["ypart1"], sl["ygot1"])
-        h_own = (h_own.astype(F32) + delta).astype(BF)
-        stats, near, _ = norm_send(net, h_own, sl["hx_m"], sl["ssq_m"])
-        window(wn)
-        wn += 1
-        w = weight("win", l)
-        inv = norm_scale(stats, sl["ssq_m"], model_dim)
-        near.wait_recv()
-        xn = normed(sl["hx_m"].at[0], inv, columns(gx, layers + l))
-        r = w.shape[1] // 4
-        y = tdot(w[...], xn).astype(BF)
-        for d in range(4):
-            sl["upart"][slot_of(d)] = y[d * r:(d + 1) * r]
-        u = sl["u"]
-        half = [pl.ds(n * (r // 2), r // 2) for n in range(2)]
-        pieces = [[sl[k].at[:, h] for k in ("upart", "ugot")] + [sl[k].at[h] for k in ("uout", "uback")] for h in half]
-        first = [rs_first(net, part, got) for part, got, out, back in pieces]
-        second = [rs_second(net, first[n], *p) for n, p in enumerate(pieces)]
-        sent = []
-        for n, (part, got, out, back) in enumerate(pieces):
-            up = rs_last(net, second[n], part, got, back).astype(BF)
-            u[net.i, half[n]] = jax.nn.gelu(up.astype(F32)).astype(BF)
-            sent.append(gather_x(net, u.at[:, half[n]]))
-        window(wn)
-        wn += 1
-        w = weight("wout", l)
-        fwd = [gather_forward(net, u.at[:, half[n]], sent[n][1]) for n in range(2)]
-        for n in range(2):
-            sent[n][0].wait_recv()
-            fwd[n].wait_recv()
-        delta = sum_yz(net, w, u[...].reshape(-1, u.shape[2]), sl["ypart2"], sl["ygot2"])
-        h_own = (h_own.astype(F32) + delta).astype(BF)
-        end = l == layers - 1
-        stats, near, fars = norm_send(net, h_own, s[f"hx_a{l + 1}"], s[f"ssq_a{l + 1}"], far=end)
-        window(wn)
-        wn += 1
-    s["h"][...] = h_own.astype(F32).T.astype(BF)
+    h_last = [None] * HALVES
+    final = []
+    hb = s["ssq_a00"].shape[2]
+    blk = h_in.shape[0]
+    width = s["q"].shape[1]
+    waited = {}
+
+    def once(name, l):
+        if (name, l) not in waited:
+            for c in loads[name, l]:
+                c.wait()
+            waited[name, l] = s[f"{name}{l}"]
+        return waited[name, l]
+
+    def chain(h):
+        lanes = slice(h * hb, (h + 1) * hb)
+        seqs = pl.ds(h * hb, hb)
+        h_own = h_in[:, lanes]
+        stats, near, _ = norm_send(net, h_own, s[f"hx_a0{h}"], s[f"ssq_a0{h}"])
+        head = [g_near] if h == 0 else []
+        if h == 0:
+            g_fars.extend([net.put(gx.at[net.j], gfar.at[net.j], to) for to in (net.across, net.peer(2, 1))])
+        for l in range(layers):
+            sl = {k[:-2]: s[k] for k in s if k.endswith(f"{l}{h}")}
+            yield stats + [near] + head, 0.9
+            head = []
+            inv = norm_scale(sl["ssq_a"], model_dim)
+            xn = normed(sl["hx_a"].at[0], inv, columns(gx, l))
+            w = once("wqkv", l)
+            part, got, back = sl["qkv_part"], sl["qkv_got"], sl["qkv_back"]
+            for n in range(3):
+                y = tdot(w[n], xn).astype(BF)
+                for d in range(4):
+                    part[slot_of(d), n * width:(n + 1) * width] = y[d * width:(d + 1) * width]
+            first = rs_first(net, part, got)
+            yield [first], 0.2
+            second = rs_second(net, part, got, sl["qkv_out"], back)
+            yield [second], 0.3
+            y = rs_last(net, part, got, back).astype(BF)
+            for n, dst in enumerate(("kt", "vt")):
+                s[dst][l, :, seqs] = y[(n + 1) * width:(n + 2) * width]
+            for n, dst in enumerate((kt_out, vt_out)):
+                src = s[("kt", "vt")[n]]
+                stores.append(net.fetch(src.at[l, :, seqs], dst.at[l, :, seqs]))
+            for n, dst in enumerate(("q", "k", "v")):
+                s[dst][seqs, :] = y[n * width:(n + 1) * width].astype(F32).T
+            for n in range(PARTS):
+                yield [], 17.0 / HALVES / PARTS + 0.2, (l * HALVES + h) * PARTS + n
+                att.piece(l, h, n, PARTS)
+            if l == layers - 1 and h == 0:
+                loads["wu", 0] = [net.fetch(wu, s["wu"])]
+            o = sl["o"]
+            o[net.i] = s["att"][seqs, :].T.astype(BF)
+            sib, across = gather_x(net, o)
+            yield [across], 0.1
+            fwd = gather_forward(net, o)
+            yield [sib, fwd], 0.4
+            w = once("wo", l)
+            act = o[...].reshape(-1, hb)
+            summed = send_half(net, w, act, sl["ypart1"], sl["ygot1"])
+            mine = own_half(net, w, act, blk)
+            yield [summed], 0.3
+            h_own = (h_own.astype(F32) + (mine + sl["ygot1"][...].astype(F32))).astype(BF)
+            stats, near, _ = norm_send(net, h_own, sl["hx_m"], sl["ssq_m"])
+            yield stats + [near], 0.7
+            w = once("win", l)
+            inv = norm_scale(sl["ssq_m"], model_dim)
+            xn = normed(sl["hx_m"].at[0], inv, columns(gx, layers + l))
+            r = w.shape[1] // 4
+            y = tdot(w[...], xn).astype(BF)
+            part, got, back = sl["upart"], sl["ugot"], sl["uback"]
+            for d in range(4):
+                part[slot_of(d)] = y[d * r:(d + 1) * r]
+            first = rs_first(net, part, got)
+            yield [first], 0.2
+            second = rs_second(net, part, got, sl["uout"], back)
+            yield [second], 0.4
+            up = rs_last(net, part, got, back).astype(BF)
+            u = sl["u"]
+            u[net.i] = jax.nn.gelu(up.astype(F32)).astype(BF)
+            sib, across = gather_x(net, u)
+            yield [across], 0.1
+            fwd = gather_forward(net, u)
+            yield [sib, fwd], 0.5
+            w = once("wout", l)
+            act = u[...].reshape(-1, hb)
+            summed = send_half(net, w, act, sl["ypart2"], sl["ygot2"])
+            mine = own_half(net, w, act, blk)
+            yield [summed], 0.3
+            h_own = (h_own.astype(F32) + (mine + sl["ygot2"][...].astype(F32))).astype(BF)
+            stats, near, fars = norm_send(net, h_own, s[f"hx_a{l + 1}{h}"], s[f"ssq_a{l + 1}{h}"], far=l == layers - 1)
+        s["h"][seqs, :] = h_own.astype(F32).T.astype(BF)
+        final.append((stats + [near], fars))
+
+    interleave(net, [chain(h) for h in range(HALVES)], fill)
+    while len(early) < 2 * MOVED // PIECE:
+        cross()
     stores.append(net.fetch(s["h"], h_out))
-    unembed(net, s, model_dim, 2 * layers, stats, near, fars, g_fars, early, wu_load, s[f"hx_a{layers}"], s[f"ssq_a{layers}"], p_own, p_other, stores)
+    waits = [m for f in final for m in f[0]]
+    fars = [m for f in final for m in f[1]]
+    unembed(net, s, model_dim, layers, waits, fars + g_fars + early, loads["wu", 0][0], p_own, p_other, stores)
     for c in stores:
         c.wait()
     net.finish()
 
 
-def wait_qkv(loads, s, l):
-    for c in loads.pop(("qkv", l)):
-        c.wait()
-    return s[f"wqkv{l}"]
-
-
-def unembed(net, s, model_dim, gain_row, stats, near, fars, g_fars, early, wu_load, hx, ssq, p_own, p_other, stores):
+def unembed(net, s, model_dim, layers, waits, late, wu_load, p_own, p_other, stores):
     v_loc = p_own.shape[0]
-    moved = sum(WINDOWS)
+    moved = MOVED
     left = v_loc - moved
     wu, wm, own = s["wu"], s["wm"], s["own"]
-    inv = norm_scale(stats, ssq, model_dim)
-    near.wait_recv()
-    xn = normed(hx.at[0], inv, columns(s["gx"], gain_row))
+    for c in waits:
+        c.wait_recv()
+
+    def acts(side, gains):
+        return jnp.concatenate(
+            [normed(s[f"hx_a{layers}{h}"].at[side], norm_scale(s[f"ssq_a{layers}{h}"], model_dim), columns(gains, 2 * layers))
+             for h in range(HALVES)], axis=1)
+
+    xn = acts(0, s["gx"])
     wu_load.wait()
     far_chip = 1 - net.chip
     send_a, got_a, send_b = s["send_a"], s["got_a"], s["send_b"]
@@ -426,9 +493,9 @@
     def store(a, n):
         stores.append(net.fetch(own.at[pl.ds(a, n)], p_own.at[pl.ds(a, n)]))
 
-    for c in fars + g_fars + early:
+    for c in late:
         c.wait_recv()
-    xf = normed(hx.at[1], inv, columns(s["gfar"], gain_row))
+    xf = acts(1, s["gfar"])
     x2 = jnp.concatenate([xn, xf], axis=0)
     mspans = [(a, min(512, moved - a)) for a in range(0, moved, 512)]
     send_m = s["send_m"]
@@ -476,25 +543,30 @@
 
 def scratch(layers, blk, batch, k_o, f_loc, n_qkv, v_loc, width, heads, dh, cache_len):
     r = f_loc // 4
-    moved = sum(WINDOWS)
+    moved = MOVED
     left = v_loc - moved
     t = {}
-    for l in range(layers + 1):
-        t[f"hx_a{l}"] = ((2 if l == layers else 1, 2, blk, batch), BF)
-        t[f"ssq_a{l}"] = ((8, 1, batch), F32)
+    hb = batch // HALVES
     for l in range(layers):
         t.update({
             f"wqkv{l}": ((3, 2 * blk, n_qkv), BF), f"wo{l}": ((k_o, 2 * blk), BF),
-            f"win{l}": ((2 * blk, f_loc), BF), f"wout{l}": ((f_loc, 2 * blk), BF),
-            f"qkv_part{l}": ((3, 4, width, batch), BF), f"qkv_got{l}": ((3, 2, width, batch), BF),
-            f"qkv_out{l}": ((3, width, batch), BF), f"qkv_back{l}": ((3, width, batch), BF),
-            f"o{l}": ((4, width, batch), BF),
-            f"ypart1{l}": ((blk, batch), BF), f"ygot1{l}": ((blk, batch), BF),
-            f"hx_m{l}": ((1, 2, blk, batch), BF), f"ssq_m{l}": ((8, 1, batch), F32),
-            f"upart{l}": ((4, r, batch), BF), f"ugot{l}": ((2, r, batch), BF),
-            f"uout{l}": ((r, batch), BF), f"uback{l}": ((r, batch), BF), f"u{l}": ((4, r, batch), BF),
-            f"ypart2{l}": ((blk, batch), BF), f"ygot2{l}": ((blk, batch), BF),
-        })
+            f"win{l}": ((2 * blk, f_loc), BF), f"wout{l}": ((f_loc, 2 * blk), BF)})
+    for h in range(HALVES):
+        for l in range(layers + 1):
+            t[f"hx_a{l}{h}"] = ((2 if l == layers else 1, 2, blk, hb), BF)
+            t[f"ssq_a{l}{h}"] = ((8, 1, hb), F32)
+        for l in range(layers):
+            e = f"{l}{h}"
+            t.update({
+                "qkv_part" + e: ((4, 3 * width, hb), BF), "qkv_got" + e: ((2, 3 * width, hb), BF),
+                "qkv_out" + e: ((3 * width, hb), BF), "qkv_back" + e: ((3 * width, hb), BF),
+                "o" + e: ((4, width, hb), BF),
+                "ypart1" + e: ((blk, hb), BF), "ygot1" + e: ((blk, hb), BF),
+                "hx_m" + e: ((1, 2, blk, hb), BF), "ssq_m" + e: ((8, 1, hb), F32),
+                "upart" + e: ((4, r, hb), BF), "ugot" + e: ((2, r, hb), BF),
+                "uout" + e: ((r, hb), BF), "uback" + e: ((r, hb), BF), "u" + e: ((4, r, hb), BF),
+                "ypart2" + e: ((blk, hb), BF), "ygot2" + e: ((blk, hb), BF),
+            })
     t.update({
         "gx": ((2, 8, blk), F32), "gfar": ((2, 8, blk), F32),
         "q": ((batch, width), F32), "k": ((batch, width), F32), "v": ((batch, width), F32), "att": ((batch, width), F32),

time: 143 us -> 151 us (1.056)
  Pallas kernels: 142 us -> 150 us
    pallas_call x1, Pallas kernels: 139 us -> 146 us  [decode_step(): pl.pallas_call(functools.partial(kernel, tuple(names), 8 * blk), name='de...]
where the time goes in v4:
time: 151 us
  Pallas kernels  150 us (99%)
    pallas_call x1, Pallas kernels, decode_step(): pl.pallas_call(functools.partial(kernel, tuple(names), 8 * blk), name='de...  146 us
    pallas_call x1, Pallas kernels, decode_step(): pl.pallas_call(output_kernel, name='outputs', out_shape=[sds((v_loc, batc...  3.69 us

profile of v4, /device:TPU:0, one launch (start us, length us, event | category | flops | bytes accessed | tf_op | source)
XLA Modules:
  0.0 150.9 jit_solution(3375165721053672910)
XLA Ops:
  0.6 146.4 %decode.1 = (bf16[256,128]{1,0:T(8,128)(2,1)}, bf16[4016,256]{1,0:T(8,128)(2,1)}, bf16[4016,256]{1,0:T(8,128)(2,1)}, bf16[2,128,256]{2,1,0:T(8,128)(2,1)}, bf16[2,128,256]{2,1,0:T(8,128)(2,1)}) custom-call(bf16[256,128]{1,0:T(8,128)(2,1)} %h_ref.1, s32[256]{0:T(256)} %lens_ref.1, bf16[2,256,2,64,512]{4,3,2,1,0:T(8,128)(2,1)} %bitcast.kc, ...), custom_call_target="tpu_custom_call" | custom-call | tf_op jit(solution)/shard_map/decode/pallas_call | solution.py:597
  147.0 3.7 %outputs.1 = (f32[4016,256]{1,0:T(8,128)}, bf16[256,128]{1,0:T(8,128)(2,1)}, bf16[2,128,256]{2,1,0:T(8,128)(2,1)}, bf16[2,128,256]{2,1,0:T(8,128)(2,1)}) custom-call(bf16[4016,256]{1,0:T(8,128)(2,1)} %get-tuple-element.13.p_own, bf16[4016,256]{1,0:T(8,128)(2,1)} %get-tuple-element.14.p_other, bf16[256,128]{1,0:T(8,128)(2,1)} %get-tuple-element.15.h, ...), custom_call_target="tpu_custom_call" | custom-call | tf_op jit(solution)/shard_map/outputs/pallas_call | solution.py:610

commit v5 on v4

--- a/solution.py
+++ b/solution.py
@@ -17,9 +17,10 @@
 SLOTS = 5
 HALVES = 2
 PARTS = 4
-MOVED = 3168
-PIECE = 96
-COPIES = 250
+MOVED = 3024
+PIECE = 48
+SLACK = 0.3
+COPIES = 300
 OUT_ROWS = 512
 
 
@@ -324,10 +325,7 @@
     cost = PIECE * 512 / 46e3
 
     def fill(until):
-        while len(early) < 2 * MOVED // PIECE and net.free["x"] + cost <= until:
-            net.free["x"] = max(net.free["x"], net.now)
-            if net.free["x"] + cost > until:
-                break
+        while len(early) < 2 * MOVED // PIECE and max(net.free["x"], net.now) + cost <= until + SLACK:
             cross()
 
     gx, gfar = s["gx"], s["gfar"]

time: 151 us -> 138 us (0.914)
  Pallas kernels: 150 us -> 137 us
    pallas_call x1, Pallas kernels: 146 us -> 134 us  [decode_step(): pl.pallas_call(functools.partial(kernel, tuple(names), 8 * blk), name='de...]
where the time goes in v5:
time: 138 us
  Pallas kernels  137 us (99%)
    pallas_call x1, Pallas kernels, decode_step(): pl.pallas_call(functools.partial(kernel, tuple(names), 8 * blk), name='de...  134 us
    pallas_call x1, Pallas kernels, decode_step(): pl.pallas_call(output_kernel, name='outputs', out_shape=[sds((v_loc, batc...  3.69 us

profile of v5, /device:TPU:0, one launch (start us, length us, event | category | flops | bytes accessed | tf_op | source)
XLA Modules:
  0.0 138.2 jit_solution(8659326084331557357)
XLA Ops:
  0.6 133.7 %decode.1 = (bf16[256,128]{1,0:T(8,128)(2,1)}, bf16[4016,256]{1,0:T(8,128)(2,1)}, bf16[4016,256]{1,0:T(8,128)(2,1)}, bf16[2,128,256]{2,1,0:T(8,128)(2,1)}, bf16[2,128,256]{2,1,0:T(8,128)(2,1)}) custom-call(bf16[256,128]{1,0:T(8,128)(2,1)} %h_ref.1, s32[256]{0:T(256)} %lens_ref.1, bf16[2,256,2,64,512]{4,3,2,1,0:T(8,128)(2,1)} %bitcast.kc, ...), custom_call_target="tpu_custom_call" | custom-call | tf_op jit(solution)/shard_map/decode/pallas_call | solution.py:595
  134.3 3.7 %outputs.1 = (f32[4016,256]{1,0:T(8,128)}, bf16[256,128]{1,0:T(8,128)(2,1)}, bf16[2,128,256]{2,1,0:T(8,128)(2,1)}, bf16[2,128,256]{2,1,0:T(8,128)(2,1)}) custom-call(bf16[4016,256]{1,0:T(8,128)(2,1)} %get-tuple-element.13.p_own, bf16[4016,256]{1,0:T(8,128)(2,1)} %get-tuple-element.14.p_other, bf16[256,128]{1,0:T(8,128)(2,1)} %get-tuple-element.15.h, ...), custom_call_target="tpu_custom_call" | custom-call | tf_op jit(solution)/shard_map/outputs/pallas_call | solution.py:608

commit v6 on v5

--- a/solution.py
+++ b/solution.py
@@ -20,7 +20,7 @@
 MOVED = 3024
 PIECE = 48
 SLACK = 0.3
-COPIES = 300
+COPIES = 320
 OUT_ROWS = 512
 
 
@@ -314,7 +314,7 @@
     att.start()
 
     v_loc = p_own.shape[0]
-    early = []
+    early, pending, arrivals = [], [], []
     far_chip = 1 - net.chip
 
     def cross():
@@ -325,8 +325,13 @@
     cost = PIECE * 512 / 46e3
 
     def fill(until):
-        while len(early) < 2 * MOVED // PIECE and max(net.free["x"], net.now) + cost <= until + SLACK:
-            cross()
+        while max(net.free["x"], net.now) + cost <= until + SLACK:
+            if len(early) < 2 * MOVED // PIECE:
+                cross()
+            elif pending:
+                pending.pop(0)()
+            else:
+                break
 
     gx, gfar = s["gx"], s["gfar"]
     for n, g in enumerate((ga, gm, gf)):
@@ -338,8 +343,7 @@
     g_near = net.put(gx.at[net.j], gx.at[net.j], net.yother)
     g_fars = []
     stores = []
-    h_last = [None] * HALVES
-    final = []
+    late, done = [], [False] * HALVES
     hb = s["ssq_a00"].shape[2]
     blk = h_in.shape[0]
     width = s["q"].shape[1]
@@ -430,76 +434,76 @@
             h_own = (h_own.astype(F32) + (mine + sl["ygot2"][...].astype(F32))).astype(BF)
             stats, near, fars = norm_send(net, h_own, s[f"hx_a{l + 1}{h}"], s[f"ssq_a{l + 1}{h}"], far=l == layers - 1)
         s["h"][seqs, :] = h_own.astype(F32).T.astype(BF)
-        final.append((stats + [near], fars))
+        late.extend(fars)
+        yield stats + [near], 0.7
+        xn = normed(s[f"hx_a{layers}{h}"].at[0], norm_scale(s[f"ssq_a{layers}{h}"], model_dim), columns(gx, 2 * layers))
+        s["xn"][:, seqs] = xn
+        if "wu" not in waited:
+            loads["wu", 0][0].wait()
+            waited["wu"] = True
+        left = v_loc - MOVED
+        send_a, got_a, send_b = s[f"send_a{h}"], s[f"got_a{h}"], s[f"send_b{h}"]
+        spans = [(a, min(512, left - a)) for a in range(0, left, 512)]
+        first = []
+        for a, n in spans:
+            for chip in range(2):
+                send_a[chip, pl.ds(a, n)] = product(net, s["wu"], xn, chip, 1 - net.core, v_loc, a, n).astype(BF)
+            first.append(net.put(send_a.at[:, pl.ds(a, n)], got_a.at[:, pl.ds(a, n)], net.sib))
+        for r, (a, n) in enumerate(spans):
+            yield [first[r]], 0.3
+            y = product(net, s["wu"], xn, far_chip, net.core, v_loc, a, n)
+            send_b[pl.ds(a, n)] = (y + got_a[far_chip, pl.ds(a, n)].astype(F32)).astype(BF)
+            for b in range(a, a + n, 128):
+                rows = min(128, a + n - b)
+
+                def leave(b=b, rows=rows):
+                    arrivals.append(net.put(send_b.at[pl.ds(b, rows)], p_other.at[pl.ds(MOVED + b, rows), seqs], net.across))
+
+                pending.append(leave)
+            done[h] = r == len(spans) - 1
+            if all(done):
+                while pending:
+                    pending.pop(0)()
 
     interleave(net, [chain(h) for h in range(HALVES)], fill)
     while len(early) < 2 * MOVED // PIECE:
         cross()
     stores.append(net.fetch(s["h"], h_out))
-    waits = [m for f in final for m in f[0]]
-    fars = [m for f in final for m in f[1]]
-    unembed(net, s, model_dim, layers, waits, fars + g_fars + early, loads["wu", 0][0], p_own, p_other, stores)
+    unembed(net, s, model_dim, layers, late + g_fars + early, arrivals, p_own, p_other, stores)
     for c in stores:
         c.wait()
     net.finish()
 
 
-def unembed(net, s, model_dim, layers, waits, late, wu_load, p_own, p_other, stores):
+def wu_rows(net, wu, chip, core, v_loc, a, n):
+    return wu[pl.ds(pl.multiple_of((2 * chip + core) * v_loc + a, 16), n), :]
+
+
+def product(net, wu, xn, chip, core, v_loc, a, n):
+    return jnp.dot(wu_rows(net, wu, chip, core, v_loc, MOVED + a, n), xn, preferred_element_type=F32)
+
+
+def unembed(net, s, model_dim, layers, late, arrivals, p_own, p_other, stores):
     v_loc = p_own.shape[0]
     moved = MOVED
     left = v_loc - moved
     wu, wm, own = s["wu"], s["wm"], s["own"]
-    for c in waits:
-        c.wait_recv()
-
-    def acts(side, gains):
-        return jnp.concatenate(
-            [normed(s[f"hx_a{layers}{h}"].at[side], norm_scale(s[f"ssq_a{layers}{h}"], model_dim), columns(gains, 2 * layers))
-             for h in range(HALVES)], axis=1)
-
-    xn = acts(0, s["gx"])
-    wu_load.wait()
-    far_chip = 1 - net.chip
-    send_a, got_a, send_b = s["send_a"], s["got_a"], s["send_b"]
-
-    def rows(chip, core, a, n):
-        return wu[pl.ds(pl.multiple_of((2 * chip + core) * v_loc + a, 16), n), :]
-
-    def product(chip, core, a, n):
-        return jnp.dot(rows(chip, core, moved + a, n), xn, preferred_element_type=F32)
-
-    spans = [(a, min(512, left - a)) for a in range(0, left, 512)]
-    first, arrivals = [], []
-
-    def stage1(a, n):
-        for chip in range(2):
-            send_a[chip, pl.ds(a, n)] = product(chip, 1 - net.core, a, n).astype(BF)
-        first.append(net.put(send_a.at[:, pl.ds(a, n)], got_a.at[:, pl.ds(a, n)], net.sib))
-
-    def stage2(r, a, n):
-        y = product(far_chip, net.core, a, n)
-        first[r].wait_recv()
-        send_b[pl.ds(a, n)] = (y + got_a[far_chip, pl.ds(a, n)].astype(F32)).astype(BF)
-        arrivals.append(net.put(send_b.at[pl.ds(a, n)], p_other.at[pl.ds(moved + a, n)], net.across))
-
-    stage1(*spans[0])
-    for r in range(len(spans)):
-        if r + 1 < len(spans):
-            stage1(*spans[r + 1])
-        stage2(r, *spans[r])
+    xn = s["xn"][...]
 
     def store(a, n):
         stores.append(net.fetch(own.at[pl.ds(a, n)], p_own.at[pl.ds(a, n)]))
 
     for c in late:
         c.wait_recv()
-    xf = acts(1, s["gfar"])
+    xf = jnp.concatenate(
+        [normed(s[f"hx_a{layers}{h}"].at[1], norm_scale(s[f"ssq_a{layers}{h}"], model_dim), columns(s["gfar"], 2 * layers))
+         for h in range(HALVES)], axis=1)
     x2 = jnp.concatenate([xn, xf], axis=0)
     mspans = [(a, min(512, moved - a)) for a in range(0, moved, 512)]
     send_m = s["send_m"]
 
     def both(core, a, n):
-        w2 = jnp.concatenate([rows(net.chip, core, a, n), wm[core, pl.ds(a, n), :]], axis=1)
+        w2 = jnp.concatenate([wu_rows(net, wu, net.chip, core, v_loc, a, n), wm[core, pl.ds(a, n), :]], axis=1)
         return jnp.dot(w2, x2, preferred_element_type=F32)
 
     for a, n in mspans:
@@ -508,8 +512,10 @@
     for a, n in mspans:
         own[pl.ds(a, n)] = both(net.core, a, n).astype(BF)
         store(a, n)
-    for a, n in spans:
-        y = product(net.chip, net.core, a, n) + got_a[net.chip, pl.ds(a, n)].astype(F32)
+    for a in range(0, left, 512):
+        n = min(512, left - a)
+        got = jnp.concatenate([s[f"got_a{h}"][net.chip, pl.ds(a, n)] for h in range(HALVES)], axis=1)
+        y = product(net, wu, xn, net.chip, net.core, v_loc, a, n) + got.astype(F32)
         own[pl.ds(moved + a, n)] = y.astype(BF)
         store(moved + a, n)
     for c in arrivals:
@@ -550,6 +556,7 @@
             f"wqkv{l}": ((3, 2 * blk, n_qkv), BF), f"wo{l}": ((k_o, 2 * blk), BF),
             f"win{l}": ((2 * blk, f_loc), BF), f"wout{l}": ((f_loc, 2 * blk), BF)})
     for h in range(HALVES):
+        t.update({f"send_a{h}": ((2, left, hb), BF), f"got_a{h}": ((2, left, hb), BF), f"send_b{h}": ((left, hb), BF)})
         for l in range(layers + 1):
             t[f"hx_a{l}{h}"] = ((2 if l == layers else 1, 2, blk, hb), BF)
             t[f"ssq_a{l}{h}"] = ((8, 1, hb), F32)
@@ -571,8 +578,7 @@
         "kbuf": ((SLOTS, SEQ_STEP, heads, dh, cache_len), BF), "vbuf": ((SLOTS, SEQ_STEP, heads, dh, cache_len), BF),
         "pbuf": ((SEQ_STEP // 8, 16, cache_len), BF), "pnew": ((SEQ_STEP // 8, 16, width), F32),
         "wu": ((4 * v_loc, 2 * blk), BF), "wm": ((2, moved, 2 * blk), BF),
-        "send_a": ((2, left, batch), BF), "got_a": ((2, left, batch), BF),
-        "send_b": ((left, batch), BF), "send_m": ((moved, batch), BF), "own": ((v_loc, batch), BF),
+        "xn": ((2 * blk, batch), BF), "send_m": ((moved, batch), BF), "own": ((v_loc, batch), BF),
         "kt": ((layers, width, batch), BF), "vt": ((layers, width, batch), BF), "h": ((batch, blk), BF),
     })
     return t

time: 138 us -> 135 us (0.978)
  Pallas kernels: 137 us -> 134 us
    pallas_call x1, Pallas kernels: 134 us -> 131 us  [decode_step(): pl.pallas_call(functools.partial(kernel, tuple(names), 8 * blk), name='de...]
where the time goes in v6:
time: 135 us
  Pallas kernels  134 us (99%)
    pallas_call x1, Pallas kernels, decode_step(): pl.pallas_call(functools.partial(kernel, tuple(names), 8 * blk), name='de...  131 us
    pallas_call x1, Pallas kernels, decode_step(): pl.pallas_call(output_kernel, name='outputs', out_shape=[sds((v_loc, batc...  3.69 us

profile of v6, /device:TPU:0, one launch (start us, length us, event | category | flops | bytes accessed | tf_op | source)
XLA Modules:
  0.0 135.1 jit_solution(10924610674298179859)
XLA Ops:
  0.6 130.6 %decode.1 = (bf16[256,128]{1,0:T(8,128)(2,1)}, bf16[4016,256]{1,0:T(8,128)(2,1)}, bf16[4016,256]{1,0:T(8,128)(2,1)}, bf16[2,128,256]{2,1,0:T(8,128)(2,1)}, bf16[2,128,256]{2,1,0:T(8,128)(2,1)}) custom-call(bf16[256,128]{1,0:T(8,128)(2,1)} %h_ref.1, s32[256]{0:T(256)} %lens_ref.1, bf16[2,256,2,64,512]{4,3,2,1,0:T(8,128)(2,1)} %bitcast.kc, ...), custom_call_target="tpu_custom_call" | custom-call | tf_op jit(solution)/shard_map/decode/pallas_call | solution.py:601
  131.3 3.7 %outputs.1 = (f32[4016,256]{1,0:T(8,128)}, bf16[256,128]{1,0:T(8,128)(2,1)}, bf16[2,128,256]{2,1,0:T(8,128)(2,1)}, bf16[2,128,256]{2,1,0:T(8,128)(2,1)}) custom-call(bf16[4016,256]{1,0:T(8,128)(2,1)} %get-tuple-element.13.p_own, bf16[4016,256]{1,0:T(8,128)(2,1)} %get-tuple-element.14.p_other, bf16[256,128]{1,0:T(8,128)(2,1)} %get-tuple-element.15.h, ...), custom_call_target="tpu_custom_call" | custom-call | tf_op jit(solution)/shard_map/outputs/pallas_call | solution.py:614

commit v7 on v6

--- a/solution.py
+++ b/solution.py
@@ -14,12 +14,13 @@
 ANY = pl.BlockSpec(memory_space=pl.ANY)
 VM = pl.BlockSpec(memory_space=pltpu.VMEM)
 SEQ_STEP = 16
-SLOTS = 5
+SLOTS = 7
+VT = 256
 HALVES = 2
 PARTS = 4
 MOVED = 3024
 PIECE = 48
-SLACK = 0.3
+SLACK = 0.6
 COPIES = 320
 OUT_ROWS = 512
 
@@ -29,10 +30,10 @@
 
 
 class Attention:
-    def __init__(self, lens_ref, kc_ref, vc_ref, q_ref, k_ref, v_ref, o_ref, kbuf, vbuf, pbuf, pnew, sems):
+    def __init__(self, lens_ref, kc_ref, vc_ref, q_ref, k_ref, v_ref, o_ref, kbuf, vbuf, pbuf, pnew, vt, sems):
         self.lens, self.kc, self.vc = lens_ref, kc_ref, vc_ref
         self.q, self.k, self.v, self.o = q_ref, k_ref, v_ref, o_ref
-        self.kbuf, self.vbuf, self.pbuf, self.pnew, self.sems = kbuf, vbuf, pbuf, pnew, sems
+        self.kbuf, self.vbuf, self.pbuf, self.pnew, self.vt, self.sems = kbuf, vbuf, pbuf, pnew, vt, sems
         self.layers = kc_ref.shape[0]
         self.batch, self.width = q_ref.shape
         self.dh, self.cache_len = kc_ref.shape[3], kc_ref.shape[4]
@@ -93,7 +94,11 @@
         w = self.width
         for g in self.groups:
             vb = self.vbuf[slot, 8 * g:8 * g + 8].reshape(8 * w, self.cache_len)
-            mixed = lax.dot_general(self.pbuf[g], vb, (((1,), (1,)), ((), ())), preferred_element_type=F32)
+            parts = []
+            for t in range(8 * w // VT):
+                self.vt[g, t] = vb[VT * t:VT * (t + 1)].T
+                parts.append(jnp.dot(self.pbuf[g], self.vt[g, t], preferred_element_type=F32))
+            mixed = jnp.concatenate(parts, axis=1)
             o2 = jnp.zeros((16, w), F32)
             for n in range(8):
                 o2 = jnp.where(self.row == n, mixed[:, n * w:(n + 1) * w], o2)
@@ -108,7 +113,7 @@
     def refill(self, g):
         nxt = g - 2 + SLOTS
 
-        @pl.when((g >= 2) & (nxt < self.layers * self.steps))
+        @pl.when((lax.rem(g, self.steps) >= 2) & (nxt < self.layers * self.steps))
         def _():
             self.issue(nxt)
 
@@ -134,6 +139,10 @@
         lax.fori_loop(begin, end, body, 0)
         if n == count - 1:
             self.mix(end - 1, self.fetched(jnp.int32(first + end - 1), 1))
+            if end == self.steps:
+                for g in (first + end - 2 + SLOTS, first + end - 1 + SLOTS):
+                    if g < self.layers * self.steps:
+                        self.issue(jnp.int32(g))
 
 
 class Message:
@@ -305,7 +314,7 @@
     net.greet()
     mats = (("wo", wo), ("win", win), ("wout", wout))
     loads = {("wqkv", 0): [net.fetch(w.at[0], s["wqkv0"].at[n]) for n, w in enumerate((wq, wk, wv))]}
-    att = Attention(lens_ref, kc, vc, s["q"], s["k"], s["v"], s["att"], s["kbuf"], s["vbuf"], s["pbuf"], s["pnew"], kv_sems)
+    att = Attention(lens_ref, kc, vc, s["q"], s["k"], s["v"], s["att"], s["kbuf"], s["vbuf"], s["pbuf"], s["pnew"], s["vturn"], kv_sems)
     for l in range(layers):
         if l:
             loads["wqkv", l] = [net.fetch(w.at[l], s[f"wqkv{l}"].at[n]) for n, w in enumerate((wq, wk, wv))]
@@ -389,10 +398,14 @@
             for n, dst in enumerate(("q", "k", "v")):
                 s[dst][seqs, :] = y[n * width:(n + 1) * width].astype(F32).T
             for n in range(PARTS):
-                yield [], 17.0 / HALVES / PARTS + 0.2, (l * HALVES + h) * PARTS + n
+                yield [], 14.0 / HALVES / PARTS + 0.2, (l * HALVES + h) * PARTS + n
                 att.piece(l, h, n, PARTS)
             if l == layers - 1 and h == 0:
-                loads["wu", 0] = [net.fetch(wu, s["wu"])]
+                loads["wu", 0] = []
+                for c in range(2):
+                    mine = pl.ds(pl.multiple_of((2 * net.chip + c) * v_loc, 16), v_loc)
+                    other = pl.ds(pl.multiple_of((2 * far_chip + c) * v_loc + MOVED, 16), v_loc - MOVED)
+                    loads["wu", 0] += [net.fetch(wu.at[mine], s["wu"].at[c]), net.fetch(wu.at[other], s["wu_far"].at[c])]
             o = sl["o"]
             o[net.i] = s["att"][seqs, :].T.astype(BF)
             sib, across = gather_x(net, o)
@@ -439,19 +452,20 @@
         xn = normed(s[f"hx_a{layers}{h}"].at[0], norm_scale(s[f"ssq_a{layers}{h}"], model_dim), columns(gx, 2 * layers))
         s["xn"][:, seqs] = xn
         if "wu" not in waited:
-            loads["wu", 0][0].wait()
+            for c in loads["wu", 0]:
+                c.wait()
             waited["wu"] = True
         left = v_loc - MOVED
         send_a, got_a, send_b = s[f"send_a{h}"], s[f"got_a{h}"], s[f"send_b{h}"]
         spans = [(a, min(512, left - a)) for a in range(0, left, 512)]
         first = []
         for a, n in spans:
-            for chip in range(2):
-                send_a[chip, pl.ds(a, n)] = product(net, s["wu"], xn, chip, 1 - net.core, v_loc, a, n).astype(BF)
+            send_a[net.chip, pl.ds(a, n)] = product(s["wu"], xn, 1 - net.core, MOVED + a, n).astype(BF)
+            send_a[far_chip, pl.ds(a, n)] = product(s["wu_far"], xn, 1 - net.core, a, n).astype(BF)
             first.append(net.put(send_a.at[:, pl.ds(a, n)], got_a.at[:, pl.ds(a, n)], net.sib))
         for r, (a, n) in enumerate(spans):
             yield [first[r]], 0.3
-            y = product(net, s["wu"], xn, far_chip, net.core, v_loc, a, n)
+            y = product(s["wu_far"], xn, net.core, a, n)
             send_b[pl.ds(a, n)] = (y + got_a[far_chip, pl.ds(a, n)].astype(F32)).astype(BF)
             for b in range(a, a + n, 128):
                 rows = min(128, a + n - b)
@@ -475,12 +489,8 @@
     net.finish()
 
 
-def wu_rows(net, wu, chip, core, v_loc, a, n):
-    return wu[pl.ds(pl.multiple_of((2 * chip + core) * v_loc + a, 16), n), :]
-
-
-def product(net, wu, xn, chip, core, v_loc, a, n):
-    return jnp.dot(wu_rows(net, wu, chip, core, v_loc, MOVED + a, n), xn, preferred_element_type=F32)
+def product(w, xn, core, a, n):
+    return jnp.dot(w[core, pl.ds(a, n), :], xn, preferred_element_type=F32)
 
 
 def unembed(net, s, model_dim, layers, late, arrivals, p_own, p_other, stores):
@@ -503,7 +513,7 @@
     send_m = s["send_m"]
 
     def both(core, a, n):
-        w2 = jnp.concatenate([wu_rows(net, wu, net.chip, core, v_loc, a, n), wm[core, pl.ds(a, n), :]], axis=1)
+        w2 = jnp.concatenate([wu[core, pl.ds(a, n), :], wm[core, pl.ds(a, n), :]], axis=1)
         return jnp.dot(w2, x2, preferred_element_type=F32)
 
     for a, n in mspans:
@@ -515,7 +525,7 @@
     for a in range(0, left, 512):
         n = min(512, left - a)
         got = jnp.concatenate([s[f"got_a{h}"][net.chip, pl.ds(a, n)] for h in range(HALVES)], axis=1)
-        y = product(net, wu, xn, net.chip, net.core, v_loc, a, n) + got.astype(F32)
+        y = product(wu, xn, net.core, moved + a, n) + got.astype(F32)
         own[pl.ds(moved + a, n)] = y.astype(BF)
         store(moved + a, n)
     for c in arrivals:
@@ -576,8 +586,9 @@
         "gx": ((2, 8, blk), F32), "gfar": ((2, 8, blk), F32),
         "q": ((batch, width), F32), "k": ((batch, width), F32), "v": ((batch, width), F32), "att": ((batch, width), F32),
         "kbuf": ((SLOTS, SEQ_STEP, heads, dh, cache_len), BF), "vbuf": ((SLOTS, SEQ_STEP, heads, dh, cache_len), BF),
+        "vturn": ((SEQ_STEP // 8, 8 * width // VT, cache_len, VT), BF),
         "pbuf": ((SEQ_STEP // 8, 16, cache_len), BF), "pnew": ((SEQ_STEP // 8, 16, width), F32),
-        "wu": ((4 * v_loc, 2 * blk), BF), "wm": ((2, moved, 2 * blk), BF),
+        "wu": ((2, v_loc, 2 * blk), BF), "wu_far": ((2, left, 2 * blk), BF), "wm": ((2, moved, 2 * blk), BF),
         "xn": ((2 * blk, batch), BF), "send_m": ((moved, batch), BF), "own": ((v_loc, batch), BF),
         "kt": ((layers, width, batch), BF), "vt": ((layers, width, batch), BF), "h": ((batch, blk), BF),
     })

time: 135 us -> 130 us (0.963)
  Pallas kernels: 134 us -> 129 us
    pallas_call x1, Pallas kernels: 131 us -> 125 us  [decode_step(): pl.pallas_call(functools.partial(kernel, tuple(names), 8 * blk), name='de...]
where the time goes in v7:
time: 130 us
  Pallas kernels  129 us (99%)
    pallas_call x1, Pallas kernels, decode_step(): pl.pallas_call(functools.partial(kernel, tuple(names), 8 * blk), name='de...  125 us
    pallas_call x1, Pallas kernels, decode_step(): pl.pallas_call(output_kernel, name='outputs', out_shape=[sds((v_loc, batc...  3.69 us

profile of v7, /device:TPU:0, one launch (start us, length us, event | category | flops | bytes accessed | tf_op | source)
XLA Modules:
  0.0 129.8 jit_solution(5308364605060727977)
XLA Ops:
  0.6 125.2 %decode.1 = (bf16[256,128]{1,0:T(8,128)(2,1)}, bf16[4016,256]{1,0:T(8,128)(2,1)}, bf16[4016,256]{1,0:T(8,128)(2,1)}, bf16[2,128,256]{2,1,0:T(8,128)(2,1)}, bf16[2,128,256]{2,1,0:T(8,128)(2,1)}) custom-call(bf16[256,128]{1,0:T(8,128)(2,1)} %h_ref.1, s32[256]{0:T(256)} %lens_ref.1, bf16[2,256,2,64,512]{4,3,2,1,0:T(8,128)(2,1)} %bitcast.kc, ...), custom_call_target="tpu_custom_call" | custom-call | tf_op jit(solution)/shard_map/decode/pallas_call | solution.py:612
  125.9 3.7 %outputs.1 = (f32[4016,256]{1,0:T(8,128)}, bf16[256,128]{1,0:T(8,128)(2,1)}, bf16[2,128,256]{2,1,0:T(8,128)(2,1)}, bf16[2,128,256]{2,1,0:T(8,128)(2,1)}) custom-call(bf16[4016,256]{1,0:T(8,128)(2,1)} %get-tuple-element.13.p_own, bf16[4016,256]{1,0:T(8,128)(2,1)} %get-tuple-element.14.p_other, bf16[256,128]{1,0:T(8,128)(2,1)} %get-tuple-element.15.h, ...), custom_call_target="tpu_custom_call" | custom-call | tf_op jit(solution)/shard_map/outputs/pallas_call | solution.py:625

commit v8 on v7

--- a/solution.py
+++ b/solution.py
@@ -286,7 +286,7 @@
             if dx or dy:
                 stats.append(net.put(ssq.at[me], ssq.at[me], net.peer(dx, dy)))
     near = net.put(mine, hx.at[0, net.j], net.yother)
-    fars = [net.put(mine, hx.at[1, net.j], to) for to in (net.across, net.peer(2, 1))] if far else []
+    fars = [net.put(mine, hx.at[1, net.j], net.across)] if far else []
     return stats, near, fars
 
 
@@ -447,7 +447,6 @@
             h_own = (h_own.astype(F32) + (mine + sl["ygot2"][...].astype(F32))).astype(BF)
             stats, near, fars = norm_send(net, h_own, s[f"hx_a{l + 1}{h}"], s[f"ssq_a{l + 1}{h}"], far=l == layers - 1)
         s["h"][seqs, :] = h_own.astype(F32).T.astype(BF)
-        late.extend(fars)
         yield stats + [near], 0.7
         xn = normed(s[f"hx_a{layers}{h}"].at[0], norm_scale(s[f"ssq_a{layers}{h}"], model_dim), columns(gx, 2 * layers))
         s["xn"][:, seqs] = xn
@@ -463,6 +462,9 @@
             send_a[net.chip, pl.ds(a, n)] = product(s["wu"], xn, 1 - net.core, MOVED + a, n).astype(BF)
             send_a[far_chip, pl.ds(a, n)] = product(s["wu_far"], xn, 1 - net.core, a, n).astype(BF)
             first.append(net.put(send_a.at[:, pl.ds(a, n)], got_a.at[:, pl.ds(a, n)], net.sib))
+        fars[0].wait_recv()
+        block = s[f"hx_a{layers}{h}"].at[1, net.j]
+        late.append(net.put(block, block, net.yother))
         for r, (a, n) in enumerate(spans):
             yield [first[r]], 0.3
             y = product(s["wu_far"], xn, net.core, a, n)

time: 130 us -> 129 us (level)
  no operation moved by 1% of the time
where the time goes in v8:
time: 129 us
  Pallas kernels  128 us (99%)
    pallas_call x1, Pallas kernels, decode_step(): pl.pallas_call(functools.partial(kernel, tuple(names), 8 * blk), name='de...  124 us
    pallas_call x1, Pallas kernels, decode_step(): pl.pallas_call(output_kernel, name='outputs', out_shape=[sds((v_loc, batc...  3.69 us

profile of v8, /device:TPU:0, one launch (start us, length us, event | category | flops | bytes accessed | tf_op | source)
XLA Modules:
  0.0 128.5 jit_solution(8063608526148017699)
XLA Ops:
  0.6 124.0 %decode.1 = (bf16[256,128]{1,0:T(8,128)(2,1)}, bf16[4016,256]{1,0:T(8,128)(2,1)}, bf16[4016,256]{1,0:T(8,128)(2,1)}, bf16[2,128,256]{2,1,0:T(8,128)(2,1)}, bf16[2,128,256]{2,1,0:T(8,128)(2,1)}) custom-call(bf16[256,128]{1,0:T(8,128)(2,1)} %h_ref.1, s32[256]{0:T(256)} %lens_ref.1, bf16[2,256,2,64,512]{4,3,2,1,0:T(8,128)(2,1)} %bitcast.kc, ...), custom_call_target="tpu_custom_call" | custom-call | tf_op jit(solution)/shard_map/decode/pallas_call | solution.py:614
  124.7 3.7 %outputs.1 = (f32[4016,256]{1,0:T(8,128)}, bf16[256,128]{1,0:T(8,128)(2,1)}, bf16[2,128,256]{2,1,0:T(8,128)(2,1)}, bf16[2,128,256]{2,1,0:T(8,128)(2,1)}) custom-call(bf16[4016,256]{1,0:T(8,128)(2,1)} %get-tuple-element.13.p_own, bf16[4016,256]{1,0:T(8,128)(2,1)} %get-tuple-element.14.p_other, bf16[256,128]{1,0:T(8,128)(2,1)} %get-tuple-element.15.h, ...), custom_call_target="tpu_custom_call" | custom-call | tf_op jit(solution)/shard_map/outputs/pallas_call | solution.py:627
